TPU v7x, 8 devices: a whole 2x2x1 slice. The times are simulated.
8 devices in a mesh: batch: 2 (over z, y), group: 4 (over x, core).
Axes of the slice: x: 2, y: 2, z: 1, core: 2. Of those that a mesh axis runs over, the one named last changes fastest.
Arguments:
- sort_keys: float32 [16384], P(('batch', 'group')), parts along dimension 0
- seg_ids: int32 [16384], P(('batch', 'group')), parts along dimension 0
- payload: bfloat16 [16384, 2048], P(('batch', 'group')), parts along dimension 0
Outputs:
- output: bfloat16 [16384, 2048], P(('batch', 'group')), parts along dimension 0
There are 2 independent parts. A program takes and returns all parts, laid end to end along the dimension named above; each array names one.
All inputs are finite; a program needn't handle non-finite values.
Results may differ from a plain program's by a relative error of at most 0.0066963.
Values are sent between devices in bfloat16 or wider.
A program may use at most 1 GiB of HBM per device.

v0:
```python
import jax
import jax.numpy as jnp
from jax import lax
from jax.sharding import PartitionSpec as P


def combine_runs(left_part, right_part):
    left_flag, left_rows = left_part
    right_flag, right_rows = right_part
    joined = jnp.where(right_flag[..., None], right_rows, left_rows + right_rows)
    return jnp.logical_or(left_flag, right_flag), joined


def solution(mesh):
    group_size = mesh.shape['group']

    def per_device(sort_keys, seg_ids, payload):
        rows_dev = sort_keys.shape[0]
        width = payload.shape[1]
        pair_rows = rows_dev // group_size
        capacity = 2 * pair_rows
        my_index = lax.axis_index('group')
        local_pos = jnp.arange(rows_dev, dtype=jnp.int32)
        sorted_keys, sorted_seg, local_order = lax.sort((sort_keys, seg_ids, local_pos), num_keys=1)
        samples = sorted_keys.reshape(group_size, pair_rows)[:, 0]
        all_samples = lax.all_gather(samples, 'group', tiled=True)
        ordered_samples = jnp.sort(all_samples)
        splitters = ordered_samples.reshape(group_size, group_size)[1:, group_size // 2]
        inner_starts = jnp.searchsorted(sorted_keys, splitters, side='left').astype(jnp.int32)
        bucket_start = jnp.concatenate([jnp.zeros((1,), jnp.int32), inner_starts])
        bucket_end = jnp.concatenate([inner_starts, jnp.full((1,), rows_dev, jnp.int32)])
        slot_ids = jnp.arange(capacity, dtype=jnp.int32)
        src_index = bucket_start[:, None] + slot_ids[None, :]
        in_bucket = src_index < bucket_end[:, None]
        src_clip = jnp.minimum(src_index, rows_dev - 1)
        send_keys = jnp.where(in_bucket, sorted_keys[src_clip], jnp.inf)
        send_seg = jnp.where(in_bucket, sorted_seg[src_clip], -1)
        send_rows = jnp.where(in_bucket[..., None], payload[local_order[src_clip]], 0)
        recv_keys = lax.all_to_all(send_keys, 'group', 0, 0, tiled=True)
        recv_seg = lax.all_to_all(send_seg, 'group', 0, 0, tiled=True)
        recv_rows = lax.all_to_all(send_rows, 'group', 0, 0, tiled=True)
        flat_count = group_size * capacity
        flat_pos = jnp.arange(flat_count, dtype=jnp.int32)
        merged_keys, merged_seg, merge_order = lax.sort(
            (recv_keys.reshape(flat_count), recv_seg.reshape(flat_count), flat_pos),
            num_keys=1, is_stable=True)
        merged_rows = recv_rows.reshape(flat_count, width)[merge_order].astype(jnp.float32)
        seg_change = merged_seg[1:] != merged_seg[:-1]
        run_start = jnp.concatenate([jnp.ones((1,), dtype=jnp.bool_), seg_change])
        _, local_scan = lax.associative_scan(combine_runs, (run_start, merged_rows))
        valid_count = jnp.sum(merged_keys < jnp.inf).astype(jnp.int32)
        break_pos = jnp.min(jnp.where(seg_change, flat_pos[1:], flat_count))
        inner_break = (break_pos < valid_count).astype(jnp.int32)
        last_slot = valid_count - 1
        summary_ids = jnp.stack([merged_seg[0], merged_seg[last_slot], inner_break])
        tail_sum = local_scan[last_slot]
        all_ids = lax.all_gather(summary_ids, 'group')
        all_tails = lax.all_gather(tail_sum, 'group')
        first_all = all_ids[:, 0]
        last_all = all_ids[:, 1]
        break_all = all_ids[:, 2]
        dev_ids = jnp.arange(group_size, dtype=jnp.int32)
        link_bad = jnp.concatenate(
            [jnp.ones((1,), jnp.int32), (last_all[:-1] != first_all[1:]).astype(jnp.int32)])
        bad_links = jnp.cumsum(link_bad)
        bad_inner = jnp.cumsum(break_all)
        prev_index = jnp.maximum(my_index - 1, 0)
        carry_mask = (dev_ids < my_index) & (bad_links[my_index] == bad_links) & (bad_inner[prev_index] == bad_inner)
        carry_in = jnp.dot(carry_mask.astype(jnp.float32), all_tails, preferred_element_type=jnp.float32)
        head_run = flat_pos < break_pos
        final_rows = (local_scan + jnp.where(head_run[:, None], carry_in[None, :], 0.0)).astype(jnp.bfloat16)
        _, undo_merge = lax.sort((merge_order, flat_pos), num_keys=1)
        reply = final_rows[undo_merge].reshape(group_size, capacity, width)
        returned = lax.all_to_all(reply, 'group', 0, 0, tiled=True)
        _, sorted_rank = lax.sort((local_order, local_pos), num_keys=1)
        bucket_of = jnp.searchsorted(inner_starts, sorted_rank, side='right').astype(jnp.int32)
        slot_of = bucket_of * capacity + sorted_rank - bucket_start[bucket_of]
        return returned.reshape(flat_count, width)[slot_of]

    row_spec = P(('batch', 'group'))
    mat_spec = P(('batch', 'group'), None)
    return jax.shard_map(per_device, mesh=mesh, in_specs=(row_spec, row_spec, mat_spec),
                         out_specs=mat_spec, check_vma=False)
```

profile of v0, /device:TPU:0, one launch (start us, length us, event | category | flops | bytes accessed | tf_op | source)
XLA Modules:
  0.0 1737.3 jit_solution(978696067277276605)
XLA Ops:
  7.9 8.7 all-reduce.24
  18.1 8.6 while.48
  27.4 23.0 %gather_fusion.3 = f32[4096]{0:T(1024)S(1)} fusion(f32[2048]{0:T(1024)S(1)} %get-tuple-element.373, s32[4096]{0:T(1024)S(1)} %bitcast_clamp_fusion.1), kind=kCustom, calls=%fused_computation.3 | custom fusion | bytes 49152 | tf_op jit(solution)/shard_map/gather | solution.py:36
  54.4 23.0 %gather_fusion.4 = s32[4096]{0:T(1024)S(1)} fusion(s32[2048]{0:T(1024)S(1)} %get-tuple-element.155, s32[4096]{0:T(1024)S(1)} %bitcast_clamp_fusion.1), kind=kCustom, calls=%fused_computation.4 | custom fusion | bytes 49152 | tf_op jit(solution)/shard_map/gather | solution.py:37
  78.1 23.0 %gather_fusion.1 = s32[4096]{0:T(1024)S(1)} fusion(s32[2048]{0:T(1024)S(1)} %get-tuple-element.154, s32[4096]{0:T(1024)S(1)} %bitcast_clamp_fusion.1), kind=kCustom, calls=%fused_computation.1 | custom fusion | bytes 49152 | tf_op jit(solution)/shard_map/gather | solution.py:38
  101.3 35.8 %gather_fusion.2 = bf16[4096,2048]{1,0:T(8,128)(2,1)} fusion(bf16[2048,2048]{1,0:T(8,128)(2,1)} %param.9, s32[4096]{0:T(1024)S(1)} %bitcast_clamp_fusion), kind=kCustom, calls=%fused_computation.2 | custom fusion | bytes 33570816 | tf_op jit(solution)/shard_map/gather | solution.py:38
  140.3 14.0 broadcast_select_fusion.2
  154.3 7.0 all-to-all-start
  161.9 5.7 sort.89
  173.6 170.7 %all-reduce.25 = s32[12]{0:T(128)S(1)} all-reduce(s32[12]{0:T(128)S(1)} %add_dynamic-update-slice_fusion), channel_id=3, replica_groups=mesh['batch'=2,'group'=4] {'group'}, use_global_device_ids=true, to_apply=%add.25 | all-reduce | flops 12 | bytes 96
  354.7 5.8 sort.90
  363.5 39.8 %gather_fusion.5 = bf16[4096,2048]{1,0:T(8,128)(2,1)} fusion(bf16[4096,2048]{1,0:T(8,128)(2,1)} %bitcast.2, s32[4096]{0:T(1024)S(1)} %fusion.10), kind=kCustom, calls=%fused_computation.5 | custom fusion | bytes 33570816 | tf_op jit(solution)/shard_map/gather | solution.py:47
  404.6 69.6 %slice.321 = f32[2048,2048]{1,0:T(8,128)} slice(bf16[4096,2048]{1,0:T(8,128)(2,1)} %gather_fusion.5), slice={[0:4095:2], [0:2048:1]} | slice | bytes 33554432 | tf_op jit(solution)/shard_map/slice | solution.py:50
  474.3 69.7 %slice.320 = f32[2048,2048]{1,0:T(8,128)} slice(bf16[4096,2048]{1,0:T(8,128)(2,1)} %gather_fusion.5), slice={[1:4096:2], [0:2048:1]} | slice | bytes 33554432 | tf_op jit(solution)/shard_map/slice | solution.py:50
  543.9 71.1 %slice.318 = f32[2047,2048]{1,0:T(8,128)} slice(bf16[4096,2048]{1,0:T(8,128)(2,1)} %gather_fusion.5), slice={[2:4096:2], [0:2048:1]} | slice | bytes 33538048 | tf_op jit(solution)/shard_map/slice | solution.py:50
  615.0 11.5 add_select_fusion.1
  626.5 5.7 copy-done.3
  632.2 35.9 %slice.328 = f32[1024,2048]{1,0:T(8,128)} slice(f32[2048,2048]{1,0:T(8,128)} %copy-done.3), slice={[0:2047:2], [0:2048:1]} | slice | bytes 16777216 | tf_op jit(solution)/shard_map/slice | solution.py:50
  668.1 36.0 %slice.327 = f32[1024,2048]{1,0:T(8,128)} slice(f32[2048,2048]{1,0:T(8,128)} %copy-done.3), slice={[1:2048:2], [0:2048:1]} | slice | bytes 16777216 | tf_op jit(solution)/shard_map/slice | solution.py:50
  704.1 36.8 %slice.325 = f32[1023,2048]{1,0:T(8,128)} slice(f32[2048,2048]{1,0:T(8,128)} %copy-done.3), slice={[2:2048:2], [0:2048:1]} | slice | bytes 16760832 | tf_op jit(solution)/shard_map/slice | solution.py:50
  740.9 6.5 add_select_fusion.3
  750.8 18.4 %slice.335 = f32[512,2048]{1,0:T(8,128)} slice(f32[1024,2048]{1,0:T(8,128)} %copy-done.4), slice={[0:1023:2], [0:2048:1]} | slice | bytes 8388608 | tf_op jit(solution)/shard_map/slice | solution.py:50
  769.3 18.5 %slice.334 = f32[512,2048]{1,0:T(8,128)} slice(f32[1024,2048]{1,0:T(8,128)} %copy-done.4), slice={[1:1024:2], [0:2048:1]} | slice | bytes 8388608 | tf_op jit(solution)/shard_map/slice | solution.py:50
  787.7 18.9 %slice.332 = f32[511,2048]{1,0:T(8,128)} slice(f32[1024,2048]{1,0:T(8,128)} %copy-done.4), slice={[2:1024:2], [0:2048:1]} | slice | bytes 8372224 | tf_op jit(solution)/shard_map/slice | solution.py:50
  812.5 9.8 slice.342
  822.3 9.8 slice.341
  832.1 10.0 slice.339
  869.7 8.6 pad.88
  885.8 16.5 pad.89
  902.3 8.9 pad.90
  911.2 6.8 add.321
  922.9 32.2 %pad.91 = f32[1024,2048]{1,0:T(8,128)} pad(f32[512,2048]{1,0:T(8,128)} %pad_maximum_fusion.2, f32[]{:T(128)} %constant.158.clone.1), padding=0_1_1x0_0_0 | pad | bytes 12582916 | tf_op jit(solution)/shard_map/pad | solution.py:50
  955.1 32.3 %pad.92 = f32[1024,2048]{1,0:T(8,128)} pad(f32[512,2048]{1,0:T(8,128)} %add.321, f32[]{:T(128)} %constant.158.clone.1), padding=1_0_1x0_0_0 | pad | bytes 12582916 | tf_op jit(solution)/shard_map/pad | solution.py:50
  987.4 11.7 add.323
  999.0 10.1 add_select_fusion.2
  1013.5 63.9 %pad.93 = f32[2048,2048]{1,0:T(8,128)} pad(f32[1024,2048]{1,0:T(8,128)} %pad_maximum_fusion.1, f32[]{:T(128)} %constant.158.clone.1), padding=0_1_1x0_0_0 | pad | bytes 25165828 | tf_op jit(solution)/shard_map/pad | solution.py:50
  1077.4 64.1 %pad.94 = f32[2048,2048]{1,0:T(8,128)} pad(f32[1024,2048]{1,0:T(8,128)} %add.323, f32[]{:T(128)} %constant.158.clone.1), padding=1_0_1x0_0_0 | pad | bytes 25165828 | tf_op jit(solution)/shard_map/pad | solution.py:50
  1141.5 18.1 %add.325 = f32[2048,2048]{1,0:T(8,128)} add(f32[2048,2048]{1,0:T(8,128)} %pad.93, f32[2048,2048]{1,0:T(8,128)} %pad.94) | non-fusion elementwise | flops 4194304 | bytes 50331648 | tf_op jit(solution)/shard_map/add | solution.py:50
  1163.0 17.9 %add_select_fusion = f32[2047,2048]{1,0:T(8,128)} fusion(f32[2047,2048]{1,0:T(8,128)} %slice.318, f32[2048,2048]{1,0:T(8,128)} %pad.94, f32[2048,2048]{1,0:T(8,128)S(1)} %copy-done.2, pred[2047]{0:T(1024)(128)(4,1)S(1)} %copy-done.18), kind=kLoop, calls=%fused_computation.27 | loop fusion | flops 12576768 | bytes 67078144 | tf_op jit(solution)/shard_map/jit(_where)/select_n | solution.py:10
  1180.9 11.8 pad_maximum_fusion
  1192.7 127.5 %pad.95 = f32[4096,2048]{1,0:T(8,128)} pad(f32[2048,2048]{1,0:T(8,128)} %pad_maximum_fusion, f32[]{:T(128)} %constant.158.clone.1), padding=0_1_1x0_0_0 | pad | bytes 50331652 | tf_op jit(solution)/shard_map/pad | solution.py:50
  1320.2 127.0 %pad.96 = f32[4096,2048]{1,0:T(8,128)} pad(f32[2048,2048]{1,0:T(8,128)} %add.325, f32[]{:T(128)} %constant.158.clone.1), padding=1_0_1x0_0_0 | pad | bytes 50331652 | tf_op jit(solution)/shard_map/pad | solution.py:50
  1448.2 7.1 all-gather.2
  1456.1 27.8 %add_convert_fusion = bf16[4096,2048]{1,0:T(8,128)(2,1)} fusion(f32[4096,2048]{1,0:T(8,128)} %pad.95, f32[4096,2048]{1,0:T(8,128)} %pad.96, f32[2048]{0:T(1024)S(1)} %bitcast.61, pred[4096]{0:T(1024)(128)(4,1)S(1)} %copy-done.17), kind=kLoop, calls=%fused_computation.26 | loop fusion | flops 33554432 | bytes 83898368 | tf_op jit(solution)/shard_map/convert_element_type | solution.py:71
  1483.8 39.3 %gather_fusion.6 = bf16[4096,2048]{1,0:T(8,128)(2,1)} fusion(bf16[4096,2048]{1,0:T(8,128)(2,1)} %add_convert_fusion, s32[4096]{0:T(1024)S(1)} %copy-done.15), kind=kCustom, calls=%fused_computation.6 | custom fusion | bytes 33570816 | tf_op jit(solution)/shard_map/gather | solution.py:73
  1523.1 7.1 all-to-all-start.3
  1543.0 169.9 %all-to-all-done.3 = bf16[4,1024,2048]{2,1,0:T(8,128)(2,1)} async-done(((bf16[4,1024,2048]{2,1,0:T(8,128)(2,1)}), bf16[4,1024,2048]{2,1,0:T(8,128)(2,1)}, u32[]{:S(2)}, u32[]{:S(2)}) %all-to-all-start.3) | async-done | bytes 16777248 | tf_op jit(solution)/shard_map/all_to_all | solution.py:74
  1712.9 24.2 %gather_fusion.7 = bf16[2048,2048]{1,0:T(8,128)(2,1)} fusion(bf16[4096,2048]{1,0:T(8,128)(2,1)} %bitcast.19, s32[2048]{0:T(1024)S(1)} %fusion.14), kind=kCustom, calls=%fused_computation.7 | custom fusion | bytes 16785408 | tf_op jit(solution)/shard_map/gather | solution.py:78
  (308 shorter events, 119.9 us)
Async XLA Ops:
  5.6 72.5 %copy-start = (s32[2048]{0:T(1024)}, s32[2048]{0:T(1024)S(1)}, u32[]{:S(2)}) copy-start(s32[2048]{0:T(1024)S(1)} %get-tuple-element.154) | copy-start | bytes 24580
  26.8 0.5 copy-start.13
  51.1 85.9 %all-to-all-start.1 = ((f32[4,1,1024]{2,1,0:T(1,128)}), f32[4,1,1024]{2,1,0:T(1,128)S(1)}, u32[]{:S(2)}, u32[]{:S(2)}) async-start(f32[4,1,1024]{2,1,0:T(1,128)} %compare_select_fusion.10), calls=%async_computation.1 | async-start | bytes 32768 | tf_op jit(solution)/shard_map/all_to_all | solution.py:39
  137.1 17.2 all-to-all-start.2
  154.3 209.2 %all-to-all-start = ((bf16[4,1024,2048]{2,1,0:T(8,128)(2,1)}), bf16[4,1024,2048]{2,1,0:T(8,128)(2,1)}, u32[]{:S(2)}, u32[]{:S(2)}) async-start(bf16[4,1024,2048]{2,1,0:T(8,128)(2,1)} %broadcast_select_fusion.2), calls=%async_computation | async-start | bytes 33554432 | tf_op jit(solution)/shard_map/all_to_all | solution.py:41
  352.8 50.4 %copy-start.21 = (s32[4,1]{0,1:T(1,128)}, s32[4,1]{0,1:T(1,128)S(1)}, u32[]{:S(2)}) copy-start(s32[4,1]{0,1:T(1,128)S(1)} %reduce-window.6) | copy-start | bytes 52
  626.5 5.7 copy-start.3
  747.4 3.4 copy-start.4
  810.6 1.9 copy-start.7
  844.6 16.9 copy-start.9
  861.5 3.9 copy-start.12
  864.0 5.0 copy-start.11
  864.4 4.8 slice-start.3
  869.7 14.6 slice-start.2
  884.3 18.0 %copy-start.10 = (f32[256,2048]{1,0:T(8,128)S(1)}, f32[256,2048]{1,0:T(8,128)}, u32[]{:S(2)}) copy-start(f32[256,2048]{1,0:T(8,128)} %add.319) | copy-start | bytes 6291460
  911.2 6.8 copy-start.5
  911.2 6.8 copy-start.6
  911.2 8.6 copy-start.8
  919.8 0.7 slice-start.1
  987.4 11.7 copy-start.19
  999.0 10.1 slice-start
  1141.5 21.4 %copy-start.2 = (f32[2048,2048]{1,0:T(8,128)S(1)}, f32[2048,2048]{1,0:T(8,128)}, u32[]{:S(2)}) copy-start(f32[2048,2048]{1,0:T(8,128)} %pad.93) | copy-start | bytes 50331652
  1141.5 21.4 %copy-start.18 = (pred[2047]{0:T(1024)(128)(4,1)S(1)}, pred[2047]{0:T(1024)(128)(4,1)}, u32[]{:S(2)}) copy-start(pred[2047]{0:T(1024)(128)(4,1)} %slice.317) | copy-start | bytes 6145
  1163.0 17.9 %copy-start.16 = (f32[1,2048]{1,0:T(1,128)S(1)}, f32[1,2048]{1,0:T(1,128)}, u32[]{:S(2)}) copy-start(f32[1,2048]{1,0:T(1,128)} %slice.444) | copy-start | bytes 24580
  1320.2 135.0 %copy-start.20 = (pred[4]{0:T(512)(128)(4,1)S(1)}, pred[4]{0:T(512)(128)(4,1)}, u32[]{:S(2)}) copy-start(pred[4]{0:T(512)(128)(4,1)} %compare_reduce_fusion) | copy-start | bytes 16
  1320.2 135.0 %copy-start.22 = (s32[4,1]{0,1:T(1,128)S(1)}, s32[4,1]{0,1:T(1,128)}, u32[]{:S(2)}) copy-start(s32[4,1]{0,1:T(1,128)} %copy-done.21) | copy-start | bytes 52
  1320.2 135.8 %copy-start.17 = (pred[4096]{0:T(1024)(128)(4,1)S(1)}, pred[4096]{0:T(1024)(128)(4,1)}, u32[]{:S(2)}) copy-start(pred[4096]{0:T(1024)(128)(4,1)} %iota_compare_fusion) | copy-start | bytes 12292
  1456.1 27.8 %copy-start.15 = (s32[4096]{0:T(1024)S(1)}, s32[4096]{0:T(1024)}, u32[]{:S(2)}) copy-start(s32[4096]{0:T(1024)} %fusion.11) | copy-start | bytes 49156
  1523.1 7.1 copy-start.1
  1523.1 12.2 copy-start.14
  1523.1 189.8 %all-to-all-start.3 = ((bf16[4,1024,2048]{2,1,0:T(8,128)(2,1)}), bf16[4,1024,2048]{2,1,0:T(8,128)(2,1)}, u32[]{:S(2)}, u32[]{:S(2)}) async-start(bf16[4,1024,2048]{2,1,0:T(8,128)(2,1)} %bitcast.55), calls=%async_computation.3 | async-start | bytes 33554432 | tf_op jit(solution)/shard_map/all_to_all | solution.py:74
where the time goes:
time: 1760 us; the launch traced here: 1740 us
  local copies, waits for them, and re-layouts  1150 us (65%)
  other arithmetic  204 us (12%)
  blocking collectives  187 us (11%)
  waiting for transfers between devices  170 us (10%)
  starting transfers between devices  20.5 us (1%)
    pad x22, local copies, waits for them, and re-layouts, per_device(): _, local_scan = lax.associative_scan(combine_runs, (run_start, merged_rows))  484 us
    slice x80, local copies, waits for them, and re-layouts, per_device(): _, local_scan = lax.associative_scan(combine_runs, (run_start, merged_rows))  428 us
    unnamed x1, blocking collectives  171 us
    all_to_all x1, waiting for transfers between devices, per_device(): returned = lax.all_to_all(reply, 'group', 0, 0, tiled=True)  170 us
    select_n x21, other arithmetic, combine_runs(): jnp.where(right_flag[..., None], right_rows, left_rows + right_rows)  59.9 us
    add x11, other arithmetic, per_device(): _, local_scan = lax.associative_scan(combine_runs, (run_start, merged_rows))  41.9 us
    gather x1, local copies, waits for them, and re-layouts, per_device(): recv_rows.reshape(flat_count, width)[merge_order].astype(jnp.float32)  39.8 us
    gather x1, local copies, waits for them, and re-layouts, per_device(): reply = final_rows[undo_merge].reshape(group_size, capacity, width)  39.3 us
  transfers between devices with their start and end apart: 4, of which 1 were waited for; matrix products, arithmetic and copies ran while one was open for 8% of the time, Pallas kernels for 0%

commit v1 on v0

v1 whole, which is shorter than its diff:
```python
import jax
import jax.numpy as jnp
from jax import lax
from jax.experimental import pallas as pl
from jax.experimental.pallas import tpu as pltpu
from jax.sharding import PartitionSpec as P

MESH = pl.DeviceIdType.MESH
LANES = 128
COL_W = 256
LOG_N = 13
BF16_MAX = 3.3895314e38
VMEM_LIMIT = 58400000
f32, bf16 = jnp.float32, jnp.bfloat16


def expand(ref, b, q=None):
    row = ref[pl.ds(b, 1), :] if q is None else ref[q, pl.ds(b, 1), :]
    return jnp.broadcast_to(row, (LANES, LANES)).T


def sort_index():
    sub = lax.broadcasted_iota(jnp.int32, (8, LANES), 0)
    lane = lax.broadcasted_iota(jnp.int32, (8, LANES), 1)
    return sub, lane


def bitonic(arrays):
    sub, lane = sort_index()
    arrays = [list(a) for a in arrays]

    def bit(k, v):
        if k < 3:
            return bool(v >> k & 1)
        if k < 6:
            return (sub >> (k - 3) & 1) == 1
        return (lane >> (k - 6) & 1) == 1

    for size in range(1, LOG_N + 1):
        for j in reversed(range(size)):
            if j < 3:
                for v in range(8):
                    if v >> j & 1:
                        continue
                    w = v | 1 << j
                    swap = arrays[0][v] > arrays[0][w]
                    if size < LOG_N:
                        down = bit(size, v)
                        if isinstance(down, bool):
                            swap = arrays[0][v] < arrays[0][w] if down else swap
                        else:
                            swap = jnp.logical_xor(swap, down)
                    for a in arrays:
                        a[v], a[w] = jnp.where(swap, a[w], a[v]), jnp.where(swap, a[v], a[w])
                continue
            axis, d, n = (0, 1 << (j - 3), 8) if j < 6 else (1, 1 << (j - 6), LANES)
            upper = bit(j, 0)
            for v in range(8):
                other = [jnp.where(upper, pltpu.roll(a[v], d, axis), pltpu.roll(a[v], n - d, axis))
                         for a in arrays]
                keep_max = upper
                if size < LOG_N:
                    down = bit(size, v)
                    if isinstance(down, bool):
                        keep_max = jnp.logical_not(upper) if down else upper
                    else:
                        keep_max = jnp.logical_xor(upper, down)
                take = jnp.logical_xor(other[0] < arrays[0][v], keep_max)
                for a, o in zip(arrays, other):
                    a[v] = jnp.where(take, o, a[v])
    return arrays


def shifted(values, step, fill):
    sub, lane = sort_index()
    if step == 1:
        edge, first = pltpu.roll(values[7], 1, 0), sub == 0
        edge = jnp.where(first, pltpu.roll(edge, 1, 1), edge)
        edge = jnp.where(jnp.logical_and(first, lane == 0), fill, edge)
        return [edge] + values[:7]
    edge, last = pltpu.roll(values[0], 7, 0), sub == 7
    edge = jnp.where(last, pltpu.roll(edge, LANES - 1, 1), edge)
    edge = jnp.where(jnp.logical_and(last, lane == LANES - 1), fill, edge)
    return values[1:] + [edge]


def running(values, op, start, back=False):
    sub, lane = sort_index()
    seq = values[::-1] if back else values
    inc = [seq[0]]
    for x in seq[1:]:
        inc.append(op(inc[-1], x))

    def moved(x, d, axis):
        n = 8 if axis == 0 else LANES
        at = sub if axis == 0 else lane
        if back:
            return jnp.where(at < n - d, pltpu.roll(x, n - d, axis), start)
        return jnp.where(at >= d, pltpu.roll(x, d, axis), start)

    t = inc[-1]
    for d in (1, 2, 4):
        t = op(t, moved(t, d, 0))
    row = t[0:1, :] if back else t[7:8, :]
    u = jnp.broadcast_to(row, (8, LANES))
    for d in (1, 2, 4, 8, 16, 32, 64):
        u = op(u, moved(u, d, 1))
    base = op(moved(u, 1, 1), moved(t, 1, 0))
    out = [op(base, x) for x in inc]
    return out[::-1] if back else out


def cols(c):
    return pl.ds(pl.multiple_of(c * COL_W, COL_W), COL_W)


def block(i, size):
    return pl.ds(pl.multiple_of(i * size, size), size)


def loop(n, body, first=0):
    def step(i, carry):
        body(i)
        return carry
    lax.fori_loop(first, n, step, 0)


def write_mask(mask_ref, at, own_k, low, k, column):
    inside = jnp.logical_and(k <= own_k, k > low)
    to = pl.ds(pl.multiple_of(column, LANES), LANES)
    mask_ref[at, to] = jnp.where(inside, 1.0, 0.0).astype(bf16)


def row_masks(keys_ref, lows, all_keys, mask_ref):
    key_rows = keys_ref.shape[0]
    unroll = 4

    def mask_block(b):
        own_k, low = expand(keys_ref, b), expand(lows, b)

        def fill(t):
            for q in range(all_keys.shape[0]):
                for u in range(unroll):
                    row = t * unroll + u
                    write_mask(mask_ref, block(b, LANES), own_k, low, all_keys[q, pl.ds(row, 1), :],
                               (q * key_rows + row) * LANES)

        loop(key_rows // unroll, fill)

    loop(key_rows, mask_block)


def neighbours():
    batch, me = lax.axis_index('batch'), lax.axis_index('group')
    core = lax.rem(me, 2)
    return batch, me, core, me + 1 - 2 * core, lax.rem(me + 2, 4), 3 - me


def greet(devices):
    barrier = pltpu.get_barrier_semaphore()
    for dev in devices:
        pl.semaphore_signal(barrier, inc=1, device_id=dev, device_id_type=MESH)
    pl.semaphore_wait(barrier, len(devices))


def local(src, dst, sem):
    return pltpu.make_async_copy(src, dst, sem)


def remote(src, dst, ssem, rsem, dev):
    return pltpu.make_async_remote_copy(src, dst, ssem, rsem, device_id=dev, device_id_type=MESH)


def runs_kernel(keys_ref, segs_ref, x_ref, out_ref, flag_ref, lows, all_keys, land_mate, land_raw,
                land_one, land_sum, all_segs, slots, slot_keys, col_slot, flags, mask_ref, pick_ref,
                rows_buf, mid_buf, low_buf, near_buf, one_buf, sum_buf, sum_in, acc_buf, small_send,
                small_recv, raw_send, raw_recv, mate_send, mate_recv, run_send, run_recv, fwd_send,
                fwd_recv, load_sem, near_sem):
    rows, width = x_ref.shape
    key_rows = rows // LANES
    chunks = width // COL_W
    run_chunks = chunks - 1
    ones, sums = land_one.shape[1], land_sum.shape[1]
    main = ones
    tail = sums - main
    ones_at = 2 * rows
    sums_at = ones_at + 2 * ones
    tail_at = sums_at + 2 * main
    run_cols = 2 * main + LANES
    tile = 512
    inf = jnp.inf
    batch, me, core, mate, peer, diag = neighbours()
    mate, peer, diag = (batch, mate), (batch, peer), (batch, diag)
    greet((mate, peer, diag, (1 - batch, me)))

    def small(n, src, dst, dev):
        return remote(src, dst, small_send.at[n], small_recv.at[n], dev)

    key_copies = []
    for q, dev in enumerate((mate, peer, diag)):
        key_copies.append(small(2 * q, keys_ref, all_keys.at[q + 1], dev))
        key_copies.append(small(2 * q + 1, segs_ref, all_segs.at[q + 1], dev))
    for copy in key_copies:
        copy.start()

    raw = remote(x_ref.at[:, cols(0)], land_raw.at[0], raw_send.at[0], raw_recv.at[0], peer)
    raw_fwd = remote(land_raw.at[0], land_raw.at[1], raw_send.at[1], raw_recv.at[1], mate)
    raw.start()

    def near(c):
        return remote(x_ref.at[:, cols(c)], land_mate.at[:, cols(c)], mate_send.at[c],
                      mate_recv.at[c], mate)

    loop(chunks, lambda c: near(c).start(), 1)
    near(0).start()
    all_keys[0] = keys_ref[...]
    all_segs[0] = segs_ref[...]
    for copy in key_copies:
        copy.wait()

    sub, lane = sort_index()
    key_list = [all_keys[v // 2, pl.ds(v % 2 * 8, 8), :] for v in range(8)]
    seg_list = [all_segs[v // 2, pl.ds(v % 2 * 8, 8), :] for v in range(8)]
    place = [(lane * 64 + sub * 8 + v).astype(f32) for v in range(8)]
    key_list, place_list, seg_list = bitonic([key_list, place, seg_list])

    zero, one = jnp.zeros((8, LANES), f32), jnp.ones((8, LANES), f32)
    both = jnp.logical_and

    def flag(c):
        return jnp.where(c, one, zero)

    first_seg = shifted(seg_list, 1, -1)
    before_key = shifted(key_list, 1, -inf)
    starts = [flag(x != y) for x, y in zip(seg_list, first_seg)]
    low_list = running([jnp.where(x > 0, k, -inf) for x, k in zip(starts, before_key)],
                       jnp.maximum, -inf)
    mine = [flag(p - 8.0 * jnp.floor(p * 0.125) < 4.0) for p in place_list]
    mine_before, mine_after = shifted(mine, 1, 0.0), shifted(mine, -1, 0.0)
    starts_after = shifted(starts, -1, 1.0)
    leader = [flag(both(both(m > 0, x == 0), y == 0))
              for m, x, y in zip(mine, mine_after, starts_after)]
    goes_on = [both(x > 0, y == 0) for x, y in zip(mine_after, starts_after)]
    begins = [jnp.logical_or(x == 0, y > 0) for x, y in zip(mine_before, starts)]
    weight = [jnp.where(x > 0, jnp.where(y, 1.0, 4096.0), 0.0) for x, y in zip(leader, begins)]
    counted = [x - y for x, y in zip(running(weight, jnp.add, 0.0), weight)]
    stop = [jnp.where(x > 0, 2.0 * p, jnp.where(both(m > 0, jnp.logical_not(g)), 2.0 * p + 1.0, 32768.0))
            for x, p, m, g in zip(leader, place, mine, goes_on)]
    stop = running(stop, jnp.minimum, 32768.0, back=True)
    needed = [both(m > 0, x - 2.0 * jnp.floor(x * 0.5) == 0.0) for m, x in zip(mine, stop)]

    def total(values):
        v = values[0]
        for x in values[1:]:
            v = v + x
        return jnp.sum(jnp.sum(v, axis=0, keepdims=True), axis=1, keepdims=True)

    n_single = total([flag(w == 1.0) for w in weight])
    n_longer = total([flag(w == 4096.0) for w in weight])
    spill = n_longer + jnp.maximum(n_single - 2.0 * ones, 0.0)
    flags[0] = jnp.broadcast_to(jnp.where(spill > 2.0 * sums, 1.0, 0.0), (8, LANES))

    float32_slots = float(rows)
    slot_list = []
    for w, c, m in zip(weight, counted, needed):
        before_longer = jnp.floor(c * (1.0 / 4096.0))
        before_single = c - 4096.0 * before_longer
        over = float32_slots + n_longer + before_single - 2.0 * ones
        slot = jnp.where(before_single < 2.0 * ones, before_single, over)
        slot = jnp.where(w == 1.0, slot, float32_slots + before_longer)
        slot_list.append(jnp.where(m, slot, -1.0))
    _, low_list, slot_list = bitonic([place_list, low_list, slot_list])
    for v in range(2):
        lows[pl.ds(v * 8, 8), :] = low_list[v]
    for v in range(4):
        slots[v // 2, pl.ds(v % 2 * 8, 8), :] = slot_list[v]
    flag_copy = small(6, flags.at[0], flags.at[1], peer)
    flag_copy.start()

    def near_loads(c, buf, sem):
        return (local(x_ref.at[:, cols(c)], buf.at[pl.ds(0, rows), :], sem.at[0]),
                local(land_mate.at[:, cols(c)], buf.at[pl.ds(rows, rows), :], sem.at[1]))

    def start_near(c, buf, sem):
        for copy in near_loads(c, buf, sem):
            copy.start()

    def wait_near(c, buf, sem):
        for copy in near_loads(c, buf, sem):
            copy.wait()

    near(1).wait_recv()
    start_near(1, near_buf, near_sem)

    size, unroll = 32, 4
    col_slot[...] = jnp.full(col_slot.shape, -inf, f32)

    def pick_block(b):
        base = jnp.where(b < ones // size, core * ones, rows + core * sums - ones) + b * size
        want = (lax.broadcasted_iota(jnp.int32, (size, LANES), 0) + base).astype(f32)

        def step(t, top):
            for q in range(2):
                for u in range(unroll):
                    row = t * unroll + u
                    hit = slots[q, pl.ds(row, 1), :] == want
                    pick_ref[block(b, size), block(q * key_rows + row, LANES)] = jnp.where(
                        hit, 1.0, 0.0).astype(bf16)
                    top = jnp.maximum(top, jnp.where(hit, all_keys[q, pl.ds(row, 1), :], -inf))
            return top

        top = lax.fori_loop(0, key_rows // unroll, step, jnp.full((size, LANES), -inf, f32))
        col_slot[block(b, size), :] = jnp.broadcast_to(jnp.max(top, axis=1, keepdims=True),
                                                       (size, LANES))

    loop((ones + sums) // size, pick_block)

    for t in range(col_slot.shape[0] // LANES):
        slot_keys[0, pl.ds(t, 1), :] = col_slot[pl.ds(t * LANES, LANES), :].T[0:1, :]
    slot_key_copies = (small(7, slot_keys.at[0], slot_keys.at[1], peer),
                       small(8, slot_keys.at[0], slot_keys.at[2], diag))
    for copy in slot_key_copies:
        copy.start()

    parts = ((0, ones), (0, main // 2), (main // 2, main // 2), (main, tail))

    def run(e, kind):
        at = pl.ds(*parts[kind])
        buf, land = (sum_buf, land_sum) if kind else (one_buf, land_one)
        return remote(buf.at[lax.rem(e, 2), at, :], land.at[0, at, cols(e)], run_send.at[kind, e],
                      run_recv.at[kind, e], peer)

    def fwd(e, kind):
        at = pl.ds(*parts[kind])
        land = land_sum if kind else land_one
        return remote(land.at[0, at, cols(e)], land.at[1, at, cols(e)], fwd_send.at[kind, e],
                      fwd_recv.at[kind, e], mate)

    kinds = range(len(parts))

    def reduce_runs(e):
        wait_near(e + 1, near_buf, near_sem)
        slot = lax.rem(e, 2)
        one_buf[slot] = jnp.dot(pick_ref[pl.ds(0, ones), :], near_buf[...],
                                preferred_element_type=f32).astype(bf16)
        sum_buf[slot] = jnp.dot(pick_ref[pl.ds(ones, sums), :], near_buf[...],
                                preferred_element_type=f32)
        for kind in kinds:
            run(e, kind).start()

    def next_near(e):
        near(e + 1).wait_recv()
        start_near(e + 1, near_buf, near_sem)

    def reduce_first(e):
        reduce_runs(e)
        next_near(e + 1)

    loop(2, reduce_first)

    near(0).wait_recv()
    start_near(0, rows_buf, load_sem)
    row_masks(keys_ref, lows, all_keys, mask_ref)
    raw.wait_recv()
    raw_fwd.start()

    def tiles_loop(body):
        loop(rows // tile, lambda i: body(block(i, tile)))

    def dot(at, start, n, buf, offset):
        return jnp.dot(mask_ref[at, pl.ds(start, n)], buf[pl.ds(offset, n), :],
                       preferred_element_type=f32)

    def raw_load(s):
        return local(land_raw.at[s], rows_buf.at[pl.ds((2 + s) * rows, rows), :], load_sem.at[2 + s])

    raw_load(0).start()
    raw_fwd.wait_recv()
    raw_load(1).start()
    wait_near(0, rows_buf, load_sem)
    raw_load(0).wait()
    raw_load(1).wait()

    def whole(at):
        out_ref[at, cols(0)] = dot(at, 0, mask_ref.shape[1], rows_buf, 0).astype(bf16)

    tiles_loop(whole)
    start_near(1, rows_buf, load_sem)

    for copy in slot_key_copies:
        copy.wait()

    def slot_mask(b):
        own_k, low = expand(keys_ref, b), expand(lows, b)
        for s in range(2):
            for t in range((ones + main) // LANES):
                column = t * LANES + s * ones + (ones_at if t < ones // LANES else sums_at - ones)
                write_mask(mask_ref, block(b, LANES), own_k, low, slot_keys[1 + s, pl.ds(t, 1), :],
                           column)
        t = (ones + main) // LANES
        ends = [slot_keys[1 + s, pl.ds(t, 1), :] for s in range(2)]
        ends = jnp.where(lax.broadcasted_iota(jnp.int32, ends[0].shape, 1) < tail, ends[0],
                         pltpu.roll(jnp.broadcast_to(ends[1], (8, LANES)), tail, 1)[0:1, :])
        write_mask(mask_ref, block(b, LANES), own_k, low, ends, tail_at)

    loop(key_rows, slot_mask)
    pad = LANES - 2 * tail
    for buf, end in ((rows_buf, tail_at + LANES), (mid_buf, run_cols), (low_buf, run_cols)):
        buf[pl.ds(end - pad, pad), :] = jnp.zeros((pad, COL_W), bf16)

    def split(kind, s):
        lo, n = parts[kind]
        offset = (2 * main + s * tail - lo) if lo == main else s * main

        def step(i):
            at = lo + i * size
            v = sum_in[s, block(lo // size + i, size), :]
            high = jnp.clip(v, -BF16_MAX, BF16_MAX).astype(bf16)
            rest = v - high.astype(f32)
            mid = rest.astype(bf16)
            to = pl.multiple_of(at + offset, size)
            rows_buf[pl.ds(sums_at + to, size), :] = high
            mid_buf[pl.ds(to, size), :] = mid
            low_buf[pl.ds(to, size), :] = (rest - mid.astype(f32)).astype(bf16)

        loop(n // size, step)

    def run_load(e, kind, s):
        at = pl.ds(*parts[kind])
        if kind:
            src, dst = land_sum.at[s, at, cols(e)], sum_in.at[s, at, :]
        else:
            src, dst = land_one.at[s, :, cols(e)], rows_buf.at[pl.ds(ones_at + s * ones, ones), :]
        return local(src, dst, load_sem.at[2 + 2 * kind + s])

    def receive(e, kind):
        run(e, kind).wait_recv()
        fwd(e, kind).start()
        run_load(e, kind, 0).start()

    def arrive(e, kind):
        fwd(e, kind).wait_recv()
        run_load(e, kind, 1).start()

    def take(e, kind):
        for s in range(2):
            run_load(e, kind, s).wait()
            if kind:
                split(kind, s)

    def add_chunk(e):
        for kind in kinds:
            arrive(e, kind)
        wait_near(e + 1, rows_buf, load_sem)
        for kind in kinds:
            take(e, kind)

        def whole_runs(at):
            acc = dot(at, 0, tail_at + LANES, rows_buf, 0)
            acc += dot(at, sums_at, run_cols, mid_buf, 0)
            acc += dot(at, sums_at, run_cols, low_buf, 0)
            out_ref[at, cols(e + 1)] = acc.astype(bf16)

        tiles_loop(whole_runs)
        start_near(e + 2, rows_buf, load_sem)

    def steady(e):
        for kind in kinds:
            receive(e, kind)
        for kind in kinds:
            run(e, kind).wait_send()
        reduce_runs(e + 2)

        @pl.when(e + 3 < run_chunks)
        def _():
            next_near(e + 3)

        add_chunk(e)

    loop(run_chunks - 2, steady)
    flag_copy.wait()
    flags[2] = jnp.maximum(flags[0], flags[1])
    flag_all = small(9, flags.at[2], flags.at[3], (1 - batch, me))
    flag_all.start()

    last = run_chunks - 1
    for kind in kinds:
        receive(last - 1, kind)
    add_chunk(last - 1)

    wait_near(chunks - 1, rows_buf, load_sem)

    def near_rows(at):
        acc_buf[at, :] = dot(at, 0, 2 * rows, rows_buf, 0)

    tiles_loop(near_rows)
    receive(last, 0)
    receive(last, 1)
    for kind in range(2):
        arrive(last, kind)
        take(last, kind)

    def add_sums(acc, at, lo, n):
        for s in range(2):
            place = s * main + lo
            acc += dot(at, sums_at + place, n, rows_buf, sums_at + place)
            acc += dot(at, sums_at + place, n, mid_buf, place)
            acc += dot(at, sums_at + place, n, low_buf, place)
        return acc

    def first_runs(at):
        acc = acc_buf[at, :] + dot(at, ones_at, 2 * ones, rows_buf, ones_at)
        acc_buf[at, :] = add_sums(acc, at, *parts[1])

    tiles_loop(first_runs)
    receive(last, 2)
    receive(last, 3)
    arrive(last, 2)
    take(last, 2)
    arrive(last, 3)

    def second_runs(at):
        acc_buf[at, :] = add_sums(acc_buf[at, :], at, *parts[2])

    tiles_loop(second_runs)
    take(last, 3)

    def last_runs(at):
        acc = acc_buf[at, :] + dot(at, tail_at, LANES, rows_buf, tail_at)
        acc += dot(at, tail_at, LANES, mid_buf, 2 * main)
        acc += dot(at, tail_at, LANES, low_buf, 2 * main)
        out_ref[at, cols(chunks - 1)] = acc.astype(bf16)

    tiles_loop(last_runs)
    flag_all.wait()
    flag_ref[...] = jnp.maximum(flags[2], flags[3])
    raw.wait_send()
    raw_fwd.wait_send()
    loop(chunks, lambda c: near(c).wait_send())
    for kind in kinds:
        loop(run_chunks, lambda e: fwd(e, kind).wait_send())
        loop(run_chunks, lambda e: run(e, kind).wait_send(), run_chunks - 2)


def rows_kernel(keys_ref, x_ref, lows, all_keys, out_ref, land_ref, mask_ref, rows_buf, out_buf,
                send_sem, recv_sem, load_sem):
    rows, width = x_ref.shape
    chunks = width // COL_W
    tile = COL_W
    batch, _, _, mate, peer, diag = neighbours()
    mate, peer, diag = (batch, mate), (batch, peer), (batch, diag)
    greet((mate, peer, diag))

    def copy(kind, c):
        if kind < 2:
            src, dst, dev = x_ref.at[:, cols(c)], land_ref.at[kind, :, cols(c)], (mate, peer)[kind]
        else:
            src, dst, dev = land_ref.at[1, :, cols(c)], land_ref.at[2, :, cols(c)], mate
        return remote(src, dst, send_sem.at[kind, c], recv_sem.at[kind, c], dev)

    loop(chunks, lambda c: copy(1, c).start())
    loop(chunks, lambda c: copy(0, c).start())
    row_masks(keys_ref, lows, all_keys, mask_ref)

    def chunk(c):
        copy(1, c).wait_recv()
        copy(2, c).start()
        copy(0, c).wait_recv()
        copy(2, c).wait_recv()
        loads = [local(x_ref.at[:, cols(c)], rows_buf.at[pl.ds(0, rows), :], load_sem.at[0])]
        for q in range(3):
            loads.append(local(land_ref.at[q, :, cols(c)], rows_buf.at[pl.ds((q + 1) * rows, rows), :],
                               load_sem.at[q + 1]))
        for load in loads:
            load.start()
        for load in loads:
            load.wait()

        def whole(i):
            out_buf[block(i, tile), :] = jnp.dot(mask_ref[block(i, tile), :], rows_buf[...],
                                                 preferred_element_type=f32).astype(bf16)

        loop(rows // tile, whole)
        store = local(out_buf, out_ref.at[:, cols(c)], load_sem.at[0])
        store.start()
        store.wait()

    loop(chunks, chunk)
    for kind in range(3):
        loop(chunks, lambda c: copy(kind, c).wait_send())


def solution(mesh):
    dma = pltpu.SemaphoreType.DMA
    any_spec = pl.BlockSpec(memory_space=pl.ANY)
    vmem_spec = pl.BlockSpec(memory_space=pltpu.VMEM)
    shape, vmem = jax.ShapeDtypeStruct, pltpu.VMEM

    def raw_exchange(keys, payload, lows, all_keys):
        rows, width = payload.shape
        chunks = width // COL_W
        out, _ = pl.pallas_call(
            rows_kernel,
            out_shape=(shape((rows, width), bf16), shape((3, rows, width), bf16)),
            in_specs=[vmem_spec, any_spec, vmem_spec, vmem_spec],
            out_specs=(any_spec, any_spec),
            scratch_shapes=[
                vmem((rows, 4 * rows), bf16), vmem((4 * rows, COL_W), bf16), vmem((rows, COL_W), bf16),
                dma((3, chunks)), dma((3, chunks)), dma((4,)),
            ],
            compiler_params=pltpu.CompilerParams(collective_id=1, has_side_effects=True,
                                                 vmem_limit_bytes=VMEM_LIMIT),
        )(keys, payload, lows, all_keys)
        return out

    def run_exchange(keys, segs, payload):
        rows, width = payload.shape
        ones, sums = rows // 4, rows * 17 // 64
        chunks = width // COL_W
        run_w = width - COL_W
        slot_rows = 2 * ones + LANES
        sum_rows = 2 * ones + LANES
        key_shape = keys.shape
        small, kinds = 10, 4
        return pl.pallas_call(
            runs_kernel,
            out_shape=(vmem((rows, width), bf16), vmem((8, LANES), f32), vmem(key_shape, f32),
                       vmem((4,) + key_shape, f32), shape((rows, width), bf16),
                       shape((2, rows, COL_W), bf16), shape((2, ones, run_w), bf16),
                       shape((2, sums, run_w), f32)),
            in_specs=[vmem_spec, vmem_spec, any_spec],
            out_specs=(vmem_spec,) * 4 + (any_spec,) * 4,
            scratch_shapes=[
                vmem((4,) + key_shape, jnp.int32), vmem((2,) + key_shape, f32),
                vmem((3,) + key_shape, f32), vmem((slot_rows, LANES), f32), vmem((4, 8, LANES), f32),
                vmem((rows, 4 * rows), bf16), vmem((ones + sums, 2 * rows), bf16),
                vmem((4 * rows, COL_W), bf16), vmem((sum_rows, COL_W), bf16),
                vmem((sum_rows, COL_W), bf16), vmem((2 * rows, COL_W), bf16),
                vmem((2, ones, COL_W), bf16), vmem((2, sums, COL_W), f32),
                vmem((2, sums, COL_W), f32), vmem((rows, COL_W), f32),
                dma((small,)), dma((small,)), dma((2,)), dma((2,)), dma((chunks,)), dma((chunks,)),
                dma((kinds, chunks)), dma((kinds, chunks)), dma((kinds, chunks)), dma((kinds, chunks)),
                dma((small,)), dma((2,)),
            ],
            compiler_params=pltpu.CompilerParams(collective_id=0, has_side_effects=True,
                                                 vmem_limit_bytes=VMEM_LIMIT),
        )(keys, segs, payload)[:4]

    def per_device(sort_keys, seg_ids, payload):
        key_shape = (payload.shape[0] // LANES, LANES)
        keys = sort_keys.reshape(key_shape)
        out, full, lows, all_keys = run_exchange(keys, seg_ids.reshape(key_shape), payload)
        return lax.cond(full[0, 0] > 0.0, raw_exchange, lambda *_: out, keys, payload, lows, all_keys)

    row_spec = P(('batch', 'group'))
    mat_spec = P(('batch', 'group'), None)
    return jax.shard_map(per_device, mesh=mesh, in_specs=(row_spec, row_spec, mat_spec),
                         out_specs=mat_spec, check_vma=False)
```

time: 1760 us -> 174 us (0.10); the launches traced: 1740 us -> 174 us
  local copies, waits for them, and re-layouts: 1150 us -> 3.92 us
  other arithmetic: 204 us -> 0 us
  blocking collectives: 187 us -> 0 us
  waiting for transfers between devices: 170 us -> 0 us
  Pallas kernels: 0 us -> 169 us
  starting transfers between devices: 20.5 us -> 0 us
    pad x22 -> x0, local copies, waits for them, and re-layouts: 484 us -> none  [per_device(): _, local_scan = lax.associative_scan(combine_runs, (run_start, merged_rows))]
    slice x84 -> x1, local copies, waits for them, and re-layouts: 429 us -> 0.51 us  [per_device(): full[0, 0] > 0.0]
    gather x23 -> x0, local copies, waits for them, and re-layouts: 218 us -> none  [the longest x1 39.8 us: per_device(): recv_rows.reshape(flat_count, width)[merge_order].astype(jnp.float32)]
    unnamed x1 -> x0, blocking collectives: 171 us -> none
    all_to_all x4 -> x0, waiting for transfers between devices: 170 us -> none  [the longest x1 170 us: per_device(): returned = lax.all_to_all(reply, 'group', 0, 0, tiled=True)]
    pallas_call x0 -> x1, Pallas kernels: none -> 169 us  [run_exchange(): pl.pallas_call(runs_kernel, out_shape=(vmem((rows, width), bf16), vmem((8...]
    select_n x50 -> x0, other arithmetic: 79.3 us -> none  [the longest x21 59.9 us: combine_runs(): jnp.where(right_flag[..., None], right_rows, left_rows + right_rows)]
    add x23 -> x0, other arithmetic: 42 us -> none  [the longest x11 41.9 us: per_device(): _, local_scan = lax.associative_scan(combine_runs, (run_start, merged_rows))]
  transfers between devices with their start and end apart: 4 -> 0, of which waited for: 1 -> 0; matrix products, arithmetic and copies ran while one was open for 8% -> 0% of each run, Pallas kernels for 0% -> 0%
where the time goes in v1:
time: 174 us
  Pallas kernels  169 us (97%)
  local copies, waits for them, and re-layouts  3.92 us (2%)
    pallas_call x1, Pallas kernels, run_exchange(): pl.pallas_call(runs_kernel, out_shape=(vmem((rows, width), bf16), vmem((8...  169 us

profile of v1, /device:TPU:0, one launch (start us, length us, event | category | flops | bytes accessed | tf_op | source)
XLA Modules:
  0.0 173.6 jit_solution(10921197918808097290)
XLA Ops:
  0.0 0.0 copy-start
  0.0 169.0 %shard_map.39 = (bf16[2048,2048]{1,0:T(8,128)(2,1)S(1)}, f32[8,128]{1,0:T(8,128)S(1)}, f32[16,128]{1,0:T(8,128)S(1)}, f32[4,16,128]{2,1,0:T(8,128)S(1)}, bf16[20...) custom-call(f32[16,128]{1,0:T(8,128)} %bitcast.3, ...), custom_call_target="tpu_custom_call" | custom-call | tf_op jit(solution)/shard_map/pallas_call | solution.py:625
  169.0 0.5 slice.3
  170.2 0.0 copy-done
  170.2 3.4 %copy.9 = bf16[2048,2048]{1,0:T(8,128)(2,1)} copy(bf16[2048,2048]{1,0:T(8,128)(2,1)S(1)} %get-tuple-element.30) | data formatting | bytes 16777216
  (1 shorter events, 0.0 us)
Async XLA Ops:
  0.0 170.2 %copy-start = (f32[2048]{0:T(1024)S(1)}, f32[2048]{0:T(1024)}, u32[]{:S(2)}) copy-start(f32[2048]{0:T(1024)} %param.5) | copy-start | bytes 24580

commit v2 on v1

--- a/solution.py
+++ b/solution.py
@@ -292,7 +292,7 @@
     near(1).wait_recv()
     start_near(1, near_buf, near_sem)
 
-    size, unroll = 32, 4
+    size, unroll = 16, 4
     col_slot[...] = jnp.full(col_slot.shape, -inf, f32)
 
     def pick_block(b):
@@ -448,21 +448,22 @@
             if kind:
                 split(kind, s)
 
-    def add_chunk(e):
+    def arrived(e):
         for kind in kinds:
             arrive(e, kind)
         wait_near(e + 1, rows_buf, load_sem)
         for kind in kinds:
             take(e, kind)
 
-        def whole_runs(at):
+    def add_tile(e):
+        def whole_runs(i):
+            at = block(i, tile)
             acc = dot(at, 0, tail_at + LANES, rows_buf, 0)
             acc += dot(at, sums_at, run_cols, mid_buf, 0)
             acc += dot(at, sums_at, run_cols, low_buf, 0)
             out_ref[at, cols(e + 1)] = acc.astype(bf16)
 
-        tiles_loop(whole_runs)
-        start_near(e + 2, rows_buf, load_sem)
+        return whole_runs
 
     def steady(e):
         for kind in kinds:
@@ -475,7 +476,9 @@
         def _():
             next_near(e + 3)
 
-        add_chunk(e)
+        arrived(e)
+        loop(rows // tile, add_tile(e))
+        start_near(e + 2, rows_buf, load_sem)
 
     loop(run_chunks - 2, steady)
     flag_copy.wait()
@@ -484,21 +487,23 @@
     flag_all.start()
 
     last = run_chunks - 1
+
+    def near_rows(at):
+        acc_buf[at, :] = dot(at, 0, 2 * rows, near_buf, 0)
+
+    tiles_loop(near_rows)
     for kind in kinds:
         receive(last - 1, kind)
-    add_chunk(last - 1)
-
-    wait_near(chunks - 1, rows_buf, load_sem)
-
-    def near_rows(at):
-        acc_buf[at, :] = dot(at, 0, 2 * rows, rows_buf, 0)
-
-    tiles_loop(near_rows)
-    receive(last, 0)
+    arrived(last - 1)
+    half = rows // tile // 2
+    loop(half, add_tile(last - 1))
+    run(last, 0).wait_recv()
+    fwd(last, 0).start()
+    loop(2 * half, add_tile(last - 1), half)
+    run_load(last, 0, 0).start()
     receive(last, 1)
-    for kind in range(2):
-        arrive(last, kind)
-        take(last, kind)
+    arrive(last, 0)
+    take(last, 0)
 
     def add_sums(acc, at, lo, n):
         for s in range(2):
@@ -508,20 +513,24 @@
             acc += dot(at, sums_at + place, n, low_buf, place)
         return acc
 
+    def single_rows(at):
+        acc_buf[at, :] += dot(at, ones_at, 2 * ones, rows_buf, ones_at)
+
     def first_runs(at):
-        acc = acc_buf[at, :] + dot(at, ones_at, 2 * ones, rows_buf, ones_at)
-        acc_buf[at, :] = add_sums(acc, at, *parts[1])
-
+        acc_buf[at, :] = add_sums(acc_buf[at, :], at, *parts[1])
+
+    def second_runs(at):
+        acc_buf[at, :] = add_sums(acc_buf[at, :], at, *parts[2])
+
+    tiles_loop(single_rows)
+    arrive(last, 1)
+    take(last, 1)
+    receive(last, 2)
     tiles_loop(first_runs)
-    receive(last, 2)
     receive(last, 3)
     arrive(last, 2)
     take(last, 2)
     arrive(last, 3)
-
-    def second_runs(at):
-        acc_buf[at, :] = add_sums(acc_buf[at, :], at, *parts[2])
-
     tiles_loop(second_runs)
     take(last, 3)
 
@@ -615,7 +624,7 @@
 
     def run_exchange(keys, segs, payload):
         rows, width = payload.shape
-        ones, sums = rows // 4, rows * 17 // 64
+        ones, sums = rows // 4, rows * 33 // 128
         chunks = width // COL_W
         run_w = width - COL_W
         slot_rows = 2 * ones + LANES

time: 174 us -> 172 us (0.989)
  Pallas kernels: 169 us -> 167 us
    pallas_call x1, Pallas kernels: 169 us -> 167 us  [run_exchange(): pl.pallas_call(runs_kernel, out_shape=(vmem((rows, width), bf16), vmem((8...]
where the time goes in v2:
time: 172 us; the launch traced here: 171 us
  Pallas kernels  167 us (97%)
  local copies, waits for them, and re-layouts  3.92 us (2%)
    pallas_call x1, Pallas kernels, run_exchange(): pl.pallas_call(runs_kernel, out_shape=(vmem((rows, width), bf16), vmem((8...  167 us

profile of v2, /device:TPU:0, one launch (start us, length us, event | category | flops | bytes accessed | tf_op | source)
XLA Modules:
  0.0 171.3 jit_solution(17030367849966832634)
XLA Ops:
  0.0 0.0 copy-start
  0.0 166.7 %shard_map.39 = (bf16[2048,2048]{1,0:T(8,128)(2,1)S(1)}, f32[8,128]{1,0:T(8,128)S(1)}, f32[16,128]{1,0:T(8,128)S(1)}, f32[4,16,128]{2,1,0:T(8,128)S(1)}, bf16[20...) custom-call(f32[16,128]{1,0:T(8,128)} %bitcast.3, ...), custom_call_target="tpu_custom_call" | custom-call | tf_op jit(solution)/shard_map/pallas_call | solution.py:634
  166.8 0.5 slice.3
  167.9 0.0 copy-done
  167.9 3.4 %copy.9 = bf16[2048,2048]{1,0:T(8,128)(2,1)} copy(bf16[2048,2048]{1,0:T(8,128)(2,1)S(1)} %get-tuple-element.30) | data formatting | bytes 16777216
  (1 shorter events, 0.0 us)
Async XLA Ops:
  0.0 167.9 %copy-start = (f32[2048]{0:T(1024)S(1)}, f32[2048]{0:T(1024)}, u32[]{:S(2)}) copy-start(f32[2048]{0:T(1024)} %param.5) | copy-start | bytes 24580

commit v3 on v2

--- a/solution.py
+++ b/solution.py
@@ -131,7 +131,7 @@
     mask_ref[at, to] = jnp.where(inside, 1.0, 0.0).astype(bf16)
 
 
-def row_masks(keys_ref, lows, all_keys, mask_ref):
+def row_masks(keys_ref, lows, all_keys, places, between=None):
     key_rows = keys_ref.shape[0]
     unroll = 4
 
@@ -139,15 +139,20 @@
         own_k, low = expand(keys_ref, b), expand(lows, b)
 
         def fill(t):
-            for q in range(all_keys.shape[0]):
+            for q, (ref, first) in enumerate(places):
                 for u in range(unroll):
                     row = t * unroll + u
-                    write_mask(mask_ref, block(b, LANES), own_k, low, all_keys[q, pl.ds(row, 1), :],
-                               (q * key_rows + row) * LANES)
+                    write_mask(ref, block(b, LANES), own_k, low, all_keys[q, pl.ds(row, 1), :],
+                               row * LANES + first)
 
         loop(key_rows // unroll, fill)
 
-    loop(key_rows, mask_block)
+    if between is None:
+        loop(key_rows, mask_block)
+    else:
+        loop(key_rows // 2, mask_block)
+        between()
+        loop(key_rows, mask_block, key_rows // 2)
 
 
 def neighbours():
@@ -187,7 +192,7 @@
     sums_at = ones_at + 2 * ones
     tail_at = sums_at + 2 * main
     run_cols = 2 * main + LANES
-    tile = 512
+    tile = 1024
     inf = jnp.inf
     batch, me, core, mate, peer, diag = neighbours()
     mate, peer, diag = (batch, mate), (batch, peer), (batch, diag)
@@ -292,7 +297,7 @@
     near(1).wait_recv()
     start_near(1, near_buf, near_sem)
 
-    size, unroll = 16, 4
+    size, unroll = 64, 4
     col_slot[...] = jnp.full(col_slot.shape, -inf, f32)
 
     def pick_block(b):
@@ -313,7 +318,7 @@
         col_slot[block(b, size), :] = jnp.broadcast_to(jnp.max(top, axis=1, keepdims=True),
                                                        (size, LANES))
 
-    loop((ones + sums) // size, pick_block)
+    loop(pick_ref.shape[0] // size, pick_block)
 
     for t in range(col_slot.shape[0] // LANES):
         slot_keys[0, pl.ds(t, 1), :] = col_slot[pl.ds(t * LANES, LANES), :].T[0:1, :]
@@ -360,9 +365,13 @@
 
     near(0).wait_recv()
     start_near(0, rows_buf, load_sem)
-    row_masks(keys_ref, lows, all_keys, mask_ref)
-    raw.wait_recv()
-    raw_fwd.start()
+
+    def forward_raw():
+        raw.wait_recv()
+        raw_fwd.start()
+
+    places = [(mask_ref, 0), (mask_ref, rows), (mask_ref, 2 * rows), (out_ref, 0)]
+    row_masks(keys_ref, lows, all_keys, places, forward_raw)
 
     def tiles_loop(body):
         loop(rows // tile, lambda i: body(block(i, tile)))
@@ -382,7 +391,9 @@
     raw_load(1).wait()
 
     def whole(at):
-        out_ref[at, cols(0)] = dot(at, 0, mask_ref.shape[1], rows_buf, 0).astype(bf16)
+        acc = dot(at, 0, 3 * rows, rows_buf, 0)
+        acc += jnp.dot(out_ref[at, :], rows_buf[pl.ds(3 * rows, rows), :], preferred_element_type=f32)
+        out_ref[at, cols(0)] = acc.astype(bf16)
 
     tiles_loop(whole)
     start_near(1, rows_buf, load_sem)
@@ -399,14 +410,18 @@
                            column)
         t = (ones + main) // LANES
         ends = [slot_keys[1 + s, pl.ds(t, 1), :] for s in range(2)]
-        ends = jnp.where(lax.broadcasted_iota(jnp.int32, ends[0].shape, 1) < tail, ends[0],
+        end_lane = lax.broadcasted_iota(jnp.int32, ends[0].shape, 1)
+        ends = jnp.where(end_lane < tail, ends[0],
                          pltpu.roll(jnp.broadcast_to(ends[1], (8, LANES)), tail, 1)[0:1, :])
+        ends = jnp.where(end_lane < 2 * tail, ends, -inf)
         write_mask(mask_ref, block(b, LANES), own_k, low, ends, tail_at)
 
     loop(key_rows, slot_mask)
     pad = LANES - 2 * tail
     for buf, end in ((rows_buf, tail_at + LANES), (mid_buf, run_cols), (low_buf, run_cols)):
         buf[pl.ds(end - pad, pad), :] = jnp.zeros((pad, COL_W), bf16)
+
+    size = tail
 
     def split(kind, s):
         lo, n = parts[kind]
@@ -465,22 +480,6 @@
 
         return whole_runs
 
-    def steady(e):
-        for kind in kinds:
-            receive(e, kind)
-        for kind in kinds:
-            run(e, kind).wait_send()
-        reduce_runs(e + 2)
-
-        @pl.when(e + 3 < run_chunks)
-        def _():
-            next_near(e + 3)
-
-        arrived(e)
-        loop(rows // tile, add_tile(e))
-        start_near(e + 2, rows_buf, load_sem)
-
-    loop(run_chunks - 2, steady)
     flag_copy.wait()
     flags[2] = jnp.maximum(flags[0], flags[1])
     flag_all = small(9, flags.at[2], flags.at[3], (1 - batch, me))
@@ -491,15 +490,42 @@
     def near_rows(at):
         acc_buf[at, :] = dot(at, 0, 2 * rows, near_buf, 0)
 
-    tiles_loop(near_rows)
-    for kind in kinds:
-        receive(last - 1, kind)
-    arrived(last - 1)
-    half = rows // tile // 2
-    loop(half, add_tile(last - 1))
-    run(last, 0).wait_recv()
-    fwd(last, 0).start()
-    loop(2 * half, add_tile(last - 1), half)
+    def steady(e):
+        @pl.when(e == last - 1)
+        def _():
+            tiles_loop(near_rows)
+
+        for kind in kinds:
+            receive(e, kind)
+
+        @pl.when(e < last - 1)
+        def _():
+            for kind in kinds:
+                run(e, kind).wait_send()
+            reduce_runs(e + 2)
+
+        @pl.when(e < last - 2)
+        def _():
+            next_near(e + 3)
+
+        arrived(e)
+        add_chunk = add_tile(e)
+
+        def step(i):
+            add_chunk(i)
+
+            @pl.when(jnp.logical_and(e == last - 1, i == 0))
+            def _():
+                run(last, 0).wait_recv()
+                fwd(last, 0).start()
+
+        loop(rows // tile, step)
+
+        @pl.when(e < last - 1)
+        def _():
+            start_near(e + 2, rows_buf, load_sem)
+
+    loop(last, steady)
     run_load(last, 0, 0).start()
     receive(last, 1)
     arrive(last, 0)
@@ -569,7 +595,7 @@
 
     loop(chunks, lambda c: copy(1, c).start())
     loop(chunks, lambda c: copy(0, c).start())
-    row_masks(keys_ref, lows, all_keys, mask_ref)
+    row_masks(keys_ref, lows, all_keys, [(mask_ref, q * rows) for q in range(4)])
 
     def chunk(c):
         copy(1, c).wait_recv()
@@ -642,7 +668,7 @@
             scratch_shapes=[
                 vmem((4,) + key_shape, jnp.int32), vmem((2,) + key_shape, f32),
                 vmem((3,) + key_shape, f32), vmem((slot_rows, LANES), f32), vmem((4, 8, LANES), f32),
-                vmem((rows, 4 * rows), bf16), vmem((ones + sums, 2 * rows), bf16),
+                vmem((rows, 3 * rows + LANES), bf16), vmem((2 * ones + COL_W // 4, 2 * rows), bf16),
                 vmem((4 * rows, COL_W), bf16), vmem((sum_rows, COL_W), bf16),
                 vmem((sum_rows, COL_W), bf16), vmem((2 * rows, COL_W), bf16),
                 vmem((2, ones, COL_W), bf16), vmem((2, sums, COL_W), f32),

time: 172 us -> 165 us (0.959)
  Pallas kernels: 167 us -> 160 us
    pallas_call x1, Pallas kernels: 167 us -> 160 us  [run_exchange(): pl.pallas_call(runs_kernel, out_shape=(vmem((rows, width), bf16), vmem((8...]
where the time goes in v3:
time: 165 us
  Pallas kernels  160 us (97%)
  local copies, waits for them, and re-layouts  3.92 us (2%)
    pallas_call x1, Pallas kernels, run_exchange(): pl.pallas_call(runs_kernel, out_shape=(vmem((rows, width), bf16), vmem((8...  160 us
    unnamed x3, local copies, waits for them, and re-layouts  3.4 us

profile of v3, /device:TPU:0, one launch (start us, length us, event | category | flops | bytes accessed | tf_op | source)
XLA Modules:
  0.0 164.6 jit_solution(12585712587807506367)
XLA Ops:
  0.0 0.0 copy-start
  0.0 160.0 %shard_map.39 = (bf16[2048,2048]{1,0:T(8,128)(2,1)S(1)}, f32[8,128]{1,0:T(8,128)S(1)}, f32[16,128]{1,0:T(8,128)S(1)}, f32[4,16,128]{2,1,0:T(8,128)S(1)}, bf16[20...) custom-call(f32[16,128]{1,0:T(8,128)} %bitcast.3, ...), custom_call_target="tpu_custom_call" | custom-call | tf_op jit(solution)/shard_map/pallas_call | solution.py:660
  160.1 0.5 slice.3
  161.2 0.0 copy-done
  161.2 3.4 %copy.9 = bf16[2048,2048]{1,0:T(8,128)(2,1)} copy(bf16[2048,2048]{1,0:T(8,128)(2,1)S(1)} %get-tuple-element.30) | data formatting | bytes 16777216
  (1 shorter events, 0.0 us)
Async XLA Ops:
  0.0 161.2 %copy-start = (f32[2048]{0:T(1024)S(1)}, f32[2048]{0:T(1024)}, u32[]{:S(2)}) copy-start(f32[2048]{0:T(1024)} %param.5) | copy-start | bytes 24580

commit v4 on v3

--- a/solution.py
+++ b/solution.py
@@ -178,9 +178,9 @@
 
 def runs_kernel(keys_ref, segs_ref, x_ref, out_ref, flag_ref, lows, all_keys, land_mate, land_raw,
                 land_one, land_sum, all_segs, slots, slot_keys, col_slot, flags, mask_ref, pick_ref,
-                rows_buf, mid_buf, low_buf, near_buf, one_buf, sum_buf, sum_in, acc_buf, small_send,
+                rows_buf, mid_buf, low_buf, near_buf, last_buf, one_buf, sum_buf, sum_in, acc_buf, small_send,
                 small_recv, raw_send, raw_recv, mate_send, mate_recv, run_send, run_recv, fwd_send,
-                fwd_recv, load_sem, near_sem):
+                fwd_recv, load_sem, near_sem, last_sem):
     rows, width = x_ref.shape
     key_rows = rows // LANES
     chunks = width // COL_W
@@ -190,7 +190,9 @@
     tail = sums - main
     ones_at = 2 * rows
     sums_at = ones_at + 2 * ones
-    tail_at = sums_at + 2 * main
+    end_tile = 4
+    tile_of = ((0, 1, 5, 7), (2, 3, 6, 8))
+    tail_at = sums_at + end_tile * LANES
     run_cols = 2 * main + LANES
     tile = 1024
     inf = jnp.inf
@@ -327,7 +329,7 @@
     for copy in slot_key_copies:
         copy.start()
 
-    parts = ((0, ones), (0, main // 2), (main // 2, main // 2), (main, tail))
+    parts = ((0, ones), (main, tail), (0, 2 * LANES), (2 * LANES, LANES), (3 * LANES, LANES))
 
     def run(e, kind):
         at = pl.ds(*parts[kind])
@@ -354,7 +356,10 @@
             run(e, kind).start()
 
     def next_near(e):
-        near(e + 1).wait_recv()
+        @pl.when(e < run_chunks - 1)
+        def _():
+            near(e + 1).wait_recv()
+
         start_near(e + 1, near_buf, near_sem)
 
     def reduce_first(e):
@@ -405,7 +410,10 @@
         own_k, low = expand(keys_ref, b), expand(lows, b)
         for s in range(2):
             for t in range((ones + main) // LANES):
-                column = t * LANES + s * ones + (ones_at if t < ones // LANES else sums_at - ones)
+                if t < ones // LANES:
+                    column = ones_at + s * ones + t * LANES
+                else:
+                    column = sums_at + tile_of[s][t - ones // LANES] * LANES
                 write_mask(mask_ref, block(b, LANES), own_k, low, slot_keys[1 + s, pl.ds(t, 1), :],
                            column)
         t = (ones + main) // LANES
@@ -418,14 +426,17 @@
 
     loop(key_rows, slot_mask)
     pad = LANES - 2 * tail
-    for buf, end in ((rows_buf, tail_at + LANES), (mid_buf, run_cols), (low_buf, run_cols)):
-        buf[pl.ds(end - pad, pad), :] = jnp.zeros((pad, COL_W), bf16)
+    for buf, end in ((rows_buf, tail_at), (mid_buf, tail_at - sums_at), (low_buf, tail_at - sums_at)):
+        buf[pl.ds(end + 2 * tail, pad), :] = jnp.zeros((pad, COL_W), bf16)
 
     size = tail
 
     def split(kind, s):
         lo, n = parts[kind]
-        offset = (2 * main + s * tail - lo) if lo == main else s * main
+        if lo == main:
+            offset = end_tile * LANES + s * tail - lo
+        else:
+            offset = tile_of[s][lo // LANES] * LANES - lo
 
         def step(i):
             at = lo + i * size
@@ -473,7 +484,7 @@
     def add_tile(e):
         def whole_runs(i):
             at = block(i, tile)
-            acc = dot(at, 0, tail_at + LANES, rows_buf, 0)
+            acc = dot(at, 0, sums_at + run_cols, rows_buf, 0)
             acc += dot(at, sums_at, run_cols, mid_buf, 0)
             acc += dot(at, sums_at, run_cols, low_buf, 0)
             out_ref[at, cols(e + 1)] = acc.astype(bf16)
@@ -488,12 +499,23 @@
     last = run_chunks - 1
 
     def near_rows(at):
-        acc_buf[at, :] = dot(at, 0, 2 * rows, near_buf, 0)
+        acc_buf[at, :] = dot(at, 0, 2 * rows, last_buf, 0)
+
+    def last_ones(s):
+        return local(land_one.at[s, :, cols(last)], near_buf.at[pl.ds(s * ones, ones), :],
+                     last_sem.at[2 + s])
+
+    near(chunks - 1).wait_recv()
+    start_near(chunks - 1, last_buf, last_sem)
 
     def steady(e):
-        @pl.when(e == last - 1)
+        @pl.when(e == last - 3)
         def _():
-            tiles_loop(near_rows)
+            wait_near(chunks - 1, last_buf, last_sem)
+
+        @pl.when(jnp.logical_and(e >= last - 3, e < last - 1))
+        def _():
+            near_rows(block(e - last + 3, tile))
 
         for kind in kinds:
             receive(e, kind)
@@ -516,8 +538,10 @@
 
             @pl.when(jnp.logical_and(e == last - 1, i == 0))
             def _():
-                run(last, 0).wait_recv()
-                fwd(last, 0).start()
+                for kind in range(2):
+                    run(last, kind).wait_recv()
+                    fwd(last, kind).start()
+                last_ones(0).start()
 
         loop(rows // tile, step)
 
@@ -526,46 +550,43 @@
             start_near(e + 2, rows_buf, load_sem)
 
     loop(last, steady)
-    run_load(last, 0, 0).start()
-    receive(last, 1)
-    arrive(last, 0)
-    take(last, 0)
-
-    def add_sums(acc, at, lo, n):
-        for s in range(2):
-            place = s * main + lo
-            acc += dot(at, sums_at + place, n, rows_buf, sums_at + place)
-            acc += dot(at, sums_at + place, n, mid_buf, place)
-            acc += dot(at, sums_at + place, n, low_buf, place)
+    receive(last, 2)
+    fwd(last, 0).wait_recv()
+    last_ones(1).start()
+    run_load(last, 1, 0).start()
+    arrive(last, 1)
+    last_ones(0).wait()
+    last_ones(1).wait()
+
+    def add_sums(acc, at, first, n):
+        for buf, offset in ((rows_buf, sums_at), (mid_buf, 0), (low_buf, 0)):
+            acc += dot(at, sums_at + first * LANES, n * LANES, buf, offset + first * LANES)
         return acc
 
     def single_rows(at):
-        acc_buf[at, :] += dot(at, ones_at, 2 * ones, rows_buf, ones_at)
+        acc_buf[at, :] += dot(at, ones_at, 2 * ones, near_buf, 0)
 
     def first_runs(at):
-        acc_buf[at, :] = add_sums(acc_buf[at, :], at, *parts[1])
+        acc_buf[at, :] = add_sums(acc_buf[at, :], at, 0, end_tile + 1)
 
     def second_runs(at):
-        acc_buf[at, :] = add_sums(acc_buf[at, :], at, *parts[2])
+        acc_buf[at, :] = add_sums(acc_buf[at, :], at, tile_of[0][2], 2)
+
+    def last_runs(at):
+        out_ref[at, cols(chunks - 1)] = add_sums(acc_buf[at, :], at, tile_of[0][3], 2).astype(bf16)
 
     tiles_loop(single_rows)
-    arrive(last, 1)
     take(last, 1)
-    receive(last, 2)
-    tiles_loop(first_runs)
-    receive(last, 3)
     arrive(last, 2)
     take(last, 2)
+    receive(last, 3)
+    tiles_loop(first_runs)
     arrive(last, 3)
+    take(last, 3)
+    receive(last, 4)
     tiles_loop(second_runs)
-    take(last, 3)
-
-    def last_runs(at):
-        acc = acc_buf[at, :] + dot(at, tail_at, LANES, rows_buf, tail_at)
-        acc += dot(at, tail_at, LANES, mid_buf, 2 * main)
-        acc += dot(at, tail_at, LANES, low_buf, 2 * main)
-        out_ref[at, cols(chunks - 1)] = acc.astype(bf16)
-
+    arrive(last, 4)
+    take(last, 4)
     tiles_loop(last_runs)
     flag_all.wait()
     flag_ref[...] = jnp.maximum(flags[2], flags[3])
@@ -656,7 +677,7 @@
         slot_rows = 2 * ones + LANES
         sum_rows = 2 * ones + LANES
         key_shape = keys.shape
-        small, kinds = 10, 4
+        small, kinds = 12, 5
         return pl.pallas_call(
             runs_kernel,
             out_shape=(vmem((rows, width), bf16), vmem((8, LANES), f32), vmem(key_shape, f32),
@@ -670,12 +691,12 @@
                 vmem((3,) + key_shape, f32), vmem((slot_rows, LANES), f32), vmem((4, 8, LANES), f32),
                 vmem((rows, 3 * rows + LANES), bf16), vmem((2 * ones + COL_W // 4, 2 * rows), bf16),
                 vmem((4 * rows, COL_W), bf16), vmem((sum_rows, COL_W), bf16),
-                vmem((sum_rows, COL_W), bf16), vmem((2 * rows, COL_W), bf16),
+                vmem((sum_rows, COL_W), bf16), vmem((2 * rows, COL_W), bf16), vmem((2 * rows, COL_W), bf16),
                 vmem((2, ones, COL_W), bf16), vmem((2, sums, COL_W), f32),
                 vmem((2, sums, COL_W), f32), vmem((rows, COL_W), f32),
                 dma((small,)), dma((small,)), dma((2,)), dma((2,)), dma((chunks,)), dma((chunks,)),
                 dma((kinds, chunks)), dma((kinds, chunks)), dma((kinds, chunks)), dma((kinds, chunks)),
-                dma((small,)), dma((2,)),
+                dma((small,)), dma((2,)), dma((4,)),
             ],
             compiler_params=pltpu.CompilerParams(collective_id=0, has_side_effects=True,
                                                  vmem_limit_bytes=VMEM_LIMIT),

time: 165 us -> 164 us (level)
  no operation moved by 1% of the time
where the time goes in v4:
time: 164 us; the launch traced here: 163 us
  Pallas kernels  159 us (97%)
  local copies, waits for them, and re-layouts  3.92 us (2%)
    pallas_call x1, Pallas kernels, run_exchange(): pl.pallas_call(runs_kernel, out_shape=(vmem((rows, width), bf16), vmem((8...  159 us
    unnamed x3, local copies, waits for them, and re-layouts  3.4 us

profile of v4, /device:TPU:0, one launch (start us, length us, event | category | flops | bytes accessed | tf_op | source)
XLA Modules:
  0.0 163.5 jit_solution(16227273617980289172)
XLA Ops:
  0.0 0.0 copy-start
  0.0 158.9 %shard_map.39 = (bf16[2048,2048]{1,0:T(8,128)(2,1)S(1)}, f32[8,128]{1,0:T(8,128)S(1)}, f32[16,128]{1,0:T(8,128)S(1)}, f32[4,16,128]{2,1,0:T(8,128)S(1)}, bf16[20...) custom-call(f32[16,128]{1,0:T(8,128)} %bitcast.3, ...), custom_call_target="tpu_custom_call" | custom-call | tf_op jit(solution)/shard_map/pallas_call | solution.py:681
  158.9 0.5 slice.3
  160.1 0.0 copy-done
  160.1 3.4 %copy.9 = bf16[2048,2048]{1,0:T(8,128)(2,1)} copy(bf16[2048,2048]{1,0:T(8,128)(2,1)S(1)} %get-tuple-element.30) | data formatting | bytes 16777216
  (1 shorter events, 0.0 us)
Async XLA Ops:
  0.0 160.1 %copy-start = (f32[2048]{0:T(1024)S(1)}, f32[2048]{0:T(1024)}, u32[]{:S(2)}) copy-start(f32[2048]{0:T(1024)} %param.5) | copy-start | bytes 24580

commit v5 on v4

--- a/solution.py
+++ b/solution.py
@@ -10,7 +10,8 @@
 COL_W = 256
 LOG_N = 13
 BF16_MAX = 3.3895314e38
-VMEM_LIMIT = 58400000
+VMEM_LIMIT = 53200000
+ROWS_LIMIT = 54500000
 f32, bf16 = jnp.float32, jnp.bfloat16
 
 
@@ -176,9 +177,10 @@
     return pltpu.make_async_remote_copy(src, dst, ssem, rsem, device_id=dev, device_id_type=MESH)
 
 
-def runs_kernel(keys_ref, segs_ref, x_ref, out_ref, flag_ref, lows, all_keys, land_mate, land_raw,
+def runs_kernel(keys_ref, segs_ref, x_ref, out_ref, flag_ref, lows, all_keys, acc_buf, end_mask, end_rows,
+                land_mate, land_raw,
                 land_one, land_sum, all_segs, slots, slot_keys, col_slot, flags, mask_ref, pick_ref,
-                rows_buf, mid_buf, low_buf, near_buf, last_buf, one_buf, sum_buf, sum_in, acc_buf, small_send,
+                rows_buf, mid_buf, low_buf, near_buf, last_buf, one_buf, sum_buf, sum_in, small_send,
                 small_recv, raw_send, raw_recv, mate_send, mate_recv, run_send, run_recv, fwd_send,
                 fwd_recv, load_sem, near_sem, last_sem):
     rows, width = x_ref.shape
@@ -414,8 +416,11 @@
                     column = ones_at + s * ones + t * LANES
                 else:
                     column = sums_at + tile_of[s][t - ones // LANES] * LANES
-                write_mask(mask_ref, block(b, LANES), own_k, low, slot_keys[1 + s, pl.ds(t, 1), :],
-                           column)
+                key_row = slot_keys[1 + s, pl.ds(t, 1), :]
+                write_mask(mask_ref, block(b, LANES), own_k, low, key_row, column)
+                if column > tail_at:
+                    write_mask(end_mask, block(b, LANES), own_k, low, key_row,
+                               column - tail_at - LANES)
         t = (ones + main) // LANES
         ends = [slot_keys[1 + s, pl.ds(t, 1), :] for s in range(2)]
         end_lane = lax.broadcasted_iota(jnp.int32, ends[0].shape, 1)
@@ -569,25 +574,27 @@
     def first_runs(at):
         acc_buf[at, :] = add_sums(acc_buf[at, :], at, 0, end_tile + 1)
 
-    def second_runs(at):
-        acc_buf[at, :] = add_sums(acc_buf[at, :], at, tile_of[0][2], 2)
-
-    def last_runs(at):
-        out_ref[at, cols(chunks - 1)] = add_sums(acc_buf[at, :], at, tile_of[0][3], 2).astype(bf16)
+    def first_step(i):
+        first_runs(block(i, tile))
+
+        @pl.when(i == 0)
+        def _():
+            receive(last, 4)
 
     tiles_loop(single_rows)
     take(last, 1)
     arrive(last, 2)
     take(last, 2)
     receive(last, 3)
-    tiles_loop(first_runs)
+    loop(rows // tile, first_step)
     arrive(last, 3)
     take(last, 3)
-    receive(last, 4)
-    tiles_loop(second_runs)
     arrive(last, 4)
     take(last, 4)
-    tiles_loop(last_runs)
+    n = end_mask.shape[1]
+    from_tile = tail_at + LANES
+    for i, (buf, offset) in enumerate(((rows_buf, 0), (mid_buf, sums_at), (low_buf, sums_at))):
+        end_rows[pl.ds(i * n, n), :] = buf[pl.ds(from_tile - offset, n), :]
     flag_all.wait()
     flag_ref[...] = jnp.maximum(flags[2], flags[3])
     raw.wait_send()
@@ -598,8 +605,45 @@
         loop(run_chunks, lambda e: run(e, kind).wait_send(), run_chunks - 2)
 
 
-def rows_kernel(keys_ref, x_ref, lows, all_keys, out_ref, land_ref, mask_ref, rows_buf, out_buf,
-                send_sem, recv_sem, load_sem):
+def finish_kernel(done_ref, acc_ref, end_mask, end_rows, out_ref, last_buf, sem):
+    rows, width = done_ref.shape
+    n = end_mask.shape[1]
+    done = pl.ds(0, width - COL_W)
+    pieces = 4
+    tile = rows // 2
+
+    def store(i):
+        at = pl.ds(i * (rows // pieces), rows // pieces)
+        return local(done_ref.at[at, done], out_ref.at[at, done], sem.at[i])
+
+    def last(i):
+        at = pl.ds(i * tile, tile)
+        return local(last_buf.at[at, :], out_ref.at[at, pl.ds(width - COL_W, COL_W)],
+                     sem.at[pieces + i])
+
+    for i in range(pieces):
+        store(i).start()
+    for t in range(2):
+        at = pl.ds(t * tile, tile)
+        acc = acc_ref[at, :]
+        for i in range(3):
+            acc += jnp.dot(end_mask[at, :], end_rows[pl.ds(i * n, n), :], preferred_element_type=f32)
+        last_buf[at, :] = acc.astype(bf16)
+        last(t).start()
+    for i in range(pieces):
+        store(i).wait()
+    for t in range(2):
+        last(t).wait()
+
+
+def store_kernel(done_ref, out_ref, sem):
+    store = local(done_ref, out_ref, sem.at[0])
+    store.start()
+    store.wait()
+
+
+def rows_kernel(keys_ref, x_ref, lows, all_keys, out_ref, land_ref, mask_ref, rows_buf, send_sem,
+                recv_sem, load_sem):
     rows, width = x_ref.shape
     chunks = width // COL_W
     tile = COL_W
@@ -633,13 +677,10 @@
             load.wait()
 
         def whole(i):
-            out_buf[block(i, tile), :] = jnp.dot(mask_ref[block(i, tile), :], rows_buf[...],
-                                                 preferred_element_type=f32).astype(bf16)
+            out_ref[block(i, tile), cols(c)] = jnp.dot(mask_ref[block(i, tile), :], rows_buf[...],
+                                                       preferred_element_type=f32).astype(bf16)
 
         loop(rows // tile, whole)
-        store = local(out_buf, out_ref.at[:, cols(c)], load_sem.at[0])
-        store.start()
-        store.wait()
 
     loop(chunks, chunk)
     for kind in range(3):
@@ -652,22 +693,39 @@
     vmem_spec = pl.BlockSpec(memory_space=pltpu.VMEM)
     shape, vmem = jax.ShapeDtypeStruct, pltpu.VMEM
 
-    def raw_exchange(keys, payload, lows, all_keys):
+    def raw_exchange(keys, payload, lows, all_keys, *_):
         rows, width = payload.shape
         chunks = width // COL_W
         out, _ = pl.pallas_call(
             rows_kernel,
-            out_shape=(shape((rows, width), bf16), shape((3, rows, width), bf16)),
+            out_shape=(vmem((rows, width), bf16), shape((3, rows, width), bf16)),
             in_specs=[vmem_spec, any_spec, vmem_spec, vmem_spec],
-            out_specs=(any_spec, any_spec),
+            out_specs=(vmem_spec, any_spec),
             scratch_shapes=[
-                vmem((rows, 4 * rows), bf16), vmem((4 * rows, COL_W), bf16), vmem((rows, COL_W), bf16),
+                vmem((rows, 4 * rows), bf16), vmem((4 * rows, COL_W), bf16),
                 dma((3, chunks)), dma((3, chunks)), dma((4,)),
             ],
             compiler_params=pltpu.CompilerParams(collective_id=1, has_side_effects=True,
-                                                 vmem_limit_bytes=VMEM_LIMIT),
+                                                 vmem_limit_bytes=ROWS_LIMIT),
         )(keys, payload, lows, all_keys)
-        return out
+        return pl.pallas_call(
+            store_kernel,
+            out_shape=shape((rows, width), bf16),
+            in_specs=[vmem_spec],
+            out_specs=any_spec,
+            scratch_shapes=[dma((1,))],
+        )(out)
+
+    def finish(keys, payload, lows, all_keys, done, acc, end_mask, end_rows):
+        rows, width = payload.shape
+        return pl.pallas_call(
+            finish_kernel,
+            out_shape=shape((rows, width), bf16),
+            in_specs=[vmem_spec] * 4,
+            out_specs=any_spec,
+            scratch_shapes=[vmem((rows, COL_W), bf16), dma((6,))],
+            compiler_params=pltpu.CompilerParams(vmem_limit_bytes=16000000),
+        )(done, acc, end_mask, end_rows)
 
     def run_exchange(keys, segs, payload):
         rows, width = payload.shape
@@ -681,11 +739,13 @@
         return pl.pallas_call(
             runs_kernel,
             out_shape=(vmem((rows, width), bf16), vmem((8, LANES), f32), vmem(key_shape, f32),
-                       vmem((4,) + key_shape, f32), shape((rows, width), bf16),
+                       vmem((4,) + key_shape, f32), vmem((rows, COL_W), f32),
+                       vmem((rows, 4 * LANES), bf16), vmem((12 * LANES, COL_W), bf16),
+                       shape((rows, width), bf16),
                        shape((2, rows, COL_W), bf16), shape((2, ones, run_w), bf16),
                        shape((2, sums, run_w), f32)),
             in_specs=[vmem_spec, vmem_spec, any_spec],
-            out_specs=(vmem_spec,) * 4 + (any_spec,) * 4,
+            out_specs=(vmem_spec,) * 7 + (any_spec,) * 4,
             scratch_shapes=[
                 vmem((4,) + key_shape, jnp.int32), vmem((2,) + key_shape, f32),
                 vmem((3,) + key_shape, f32), vmem((slot_rows, LANES), f32), vmem((4, 8, LANES), f32),
@@ -693,20 +753,21 @@
                 vmem((4 * rows, COL_W), bf16), vmem((sum_rows, COL_W), bf16),
                 vmem((sum_rows, COL_W), bf16), vmem((2 * rows, COL_W), bf16), vmem((2 * rows, COL_W), bf16),
                 vmem((2, ones, COL_W), bf16), vmem((2, sums, COL_W), f32),
-                vmem((2, sums, COL_W), f32), vmem((rows, COL_W), f32),
+                vmem((2, sums, COL_W), f32),
                 dma((small,)), dma((small,)), dma((2,)), dma((2,)), dma((chunks,)), dma((chunks,)),
                 dma((kinds, chunks)), dma((kinds, chunks)), dma((kinds, chunks)), dma((kinds, chunks)),
                 dma((small,)), dma((2,)), dma((4,)),
             ],
             compiler_params=pltpu.CompilerParams(collective_id=0, has_side_effects=True,
                                                  vmem_limit_bytes=VMEM_LIMIT),
-        )(keys, segs, payload)[:4]
+        )(keys, segs, payload)[:7]
 
     def per_device(sort_keys, seg_ids, payload):
         key_shape = (payload.shape[0] // LANES, LANES)
         keys = sort_keys.reshape(key_shape)
-        out, full, lows, all_keys = run_exchange(keys, seg_ids.reshape(key_shape), payload)
-        return lax.cond(full[0, 0] > 0.0, raw_exchange, lambda *_: out, keys, payload, lows, all_keys)
+        done, full, lows, all_keys, *ends = run_exchange(keys, seg_ids.reshape(key_shape), payload)
+        return lax.cond(full[0, 0] > 0.0, raw_exchange, finish, keys, payload, lows, all_keys, done,
+                        *ends)
 
     row_spec = P(('batch', 'group'))
     mat_spec = P(('batch', 'group'), None)

time: 164 us -> 162 us (0.988)
  local copies, waits for them, and re-layouts: 3.92 us -> 0.52 us
    unnamed x3 -> x2, local copies, waits for them, and re-layouts: 3.4 us -> 0.01 us
    pallas_call x0 -> x1, Pallas kernels: none -> 3.38 us  [finish(): pl.pallas_call(finish_kernel, out_shape=shape((rows, width), bf16), in_sp...]
    pallas_call x1, Pallas kernels: 159 us -> 156 us  [run_exchange(): pl.pallas_call(runs_kernel, out_shape=(vmem((rows, width), bf16), vmem((8...]
where the time goes in v5:
time: 162 us; the launch traced here: 161 us
  Pallas kernels  160 us (99%)
    pallas_call x1, Pallas kernels, run_exchange(): pl.pallas_call(runs_kernel, out_shape=(vmem((rows, width), bf16), vmem((8...  156 us
    pallas_call x1, Pallas kernels, finish(): pl.pallas_call(finish_kernel, out_shape=shape((rows, width), bf16), in_sp...  3.38 us

profile of v5, /device:TPU:0, one launch (start us, length us, event | category | flops | bytes accessed | tf_op | source)
XLA Modules:
  0.0 161.2 jit_solution(13930948776550105001)
XLA Ops:
  0.0 0.0 copy-start.1
  0.0 156.4 %shard_map.39 = (bf16[2048,2048]{1,0:T(8,128)(2,1)S(1)}, f32[8,128]{1,0:T(8,128)S(1)}, f32[16,128]{1,0:T(8,128)S(1)}, f32[4,16,128]{2,1,0:T(8,128)S(1)}, f32[204...) custom-call(f32[16,128]{1,0:T(8,128)} %bitcast.3, ...), custom_call_target="tpu_custom_call" | custom-call | tf_op jit(solution)/shard_map/pallas_call | solution.py:739
  156.4 0.5 slice.3
  157.6 0.0 copy-done.1
  157.6 3.4 %conditional.1 = (bf16[2048,2048]{1,0:T(8,128)(2,1)}) conditional(s32[]{:T(128)} %bitcast.2, (bf16[2048,2048]{1,0:T(8,128)(2,1)S(1)}, f32[2048,256]{1,0:T(8,128)S(1)}, bf16[2048,512]{1,0:T(8,128)(2,1)S(1)}, bf16[1536,256]{1,0:T(8,128)(2,1)S(1)}) %tuple.11, (f32[16,128]{1,0:T(8,128)S(1)}, bf16[2048,2048]{1,0:T(8,128)(2,1)}, f32[16,128]{1,0:T(8,128)S(1)}, ...), branch_computations={%region_0.0_spmd, %region_1.0_spmd} | conditional | bytes 33554468 | solution.py:769
  157.6 3.4 %branch_0_fun.1 = bf16[2048,2048]{1,0:T(8,128)(2,1)} custom-call(bf16[2048,2048]{1,0:T(8,128)(2,1)S(1)} %get-tuple-element.24.done_ref, f32[2048,256]{1,0:T(8,128)S(1)} %get-tuple-element.25.acc_ref, bf16[2048,512]{1,0:T(8,128)(2,1)S(1)} %get-tuple-element.26.end_mask, bf16[1536,256]{1,0:T(8,128)(2,1)S(1)} %get-tuple-element.27.end_rows), custom_call_target="tpu_custom_call" | custom-call | tf_op jit(solution)/shard_map/cond/branch_0_fun/pallas_call | solution.py:721
Async XLA Ops:
  0.0 157.6 %copy-start.1 = (f32[2048]{0:T(1024)S(1)}, f32[2048]{0:T(1024)}, u32[]{:S(2)}) copy-start(f32[2048]{0:T(1024)} %param.5) | copy-start | bytes 24580

commit v6 on v5

--- a/solution.py
+++ b/solution.py
@@ -418,9 +418,9 @@
                     column = sums_at + tile_of[s][t - ones // LANES] * LANES
                 key_row = slot_keys[1 + s, pl.ds(t, 1), :]
                 write_mask(mask_ref, block(b, LANES), own_k, low, key_row, column)
-                if column > tail_at:
+                if t == (ones + main) // LANES - 1:
                     write_mask(end_mask, block(b, LANES), own_k, low, key_row,
-                               column - tail_at - LANES)
+                               s * LANES)
         t = (ones + main) // LANES
         ends = [slot_keys[1 + s, pl.ds(t, 1), :] for s in range(2)]
         end_lane = lax.broadcasted_iota(jnp.int32, ends[0].shape, 1)
@@ -574,12 +574,16 @@
     def first_runs(at):
         acc_buf[at, :] = add_sums(acc_buf[at, :], at, 0, end_tile + 1)
 
+    def second_runs(at):
+        acc_buf[at, :] = add_sums(acc_buf[at, :], at, tile_of[0][2], 2)
+
     def first_step(i):
         first_runs(block(i, tile))
 
         @pl.when(i == 0)
         def _():
             receive(last, 4)
+            arrive(last, 3)
 
     tiles_loop(single_rows)
     take(last, 1)
@@ -587,16 +591,16 @@
     take(last, 2)
     receive(last, 3)
     loop(rows // tile, first_step)
-    arrive(last, 3)
     take(last, 3)
+    tiles_loop(second_runs)
     arrive(last, 4)
     take(last, 4)
     n = end_mask.shape[1]
-    from_tile = tail_at + LANES
+    from_tile = sums_at + tile_of[0][3] * LANES
     for i, (buf, offset) in enumerate(((rows_buf, 0), (mid_buf, sums_at), (low_buf, sums_at))):
         end_rows[pl.ds(i * n, n), :] = buf[pl.ds(from_tile - offset, n), :]
     flag_all.wait()
-    flag_ref[...] = jnp.maximum(flags[2], flags[3])
+    flag_ref[...] = jnp.maximum(flags[2], flags[3])[0:1, 0:1]
     raw.wait_send()
     raw_fwd.wait_send()
     loop(chunks, lambda c: near(c).wait_send())
@@ -738,9 +742,9 @@
         small, kinds = 12, 5
         return pl.pallas_call(
             runs_kernel,
-            out_shape=(vmem((rows, width), bf16), vmem((8, LANES), f32), vmem(key_shape, f32),
+            out_shape=(vmem((rows, width), bf16), vmem((1, 1), f32), vmem(key_shape, f32),
                        vmem((4,) + key_shape, f32), vmem((rows, COL_W), f32),
-                       vmem((rows, 4 * LANES), bf16), vmem((12 * LANES, COL_W), bf16),
+                       vmem((rows, 2 * LANES), bf16), vmem((6 * LANES, COL_W), bf16),
                        shape((rows, width), bf16),
                        shape((2, rows, COL_W), bf16), shape((2, ones, run_w), bf16),
                        shape((2, sums, run_w), f32)),

time: 162 us -> 162 us (level)
  no operation moved by 1% of the time
where the time goes in v6:
time: 162 us
  Pallas kernels  161 us (99%)
    pallas_call x1, Pallas kernels, run_exchange(): pl.pallas_call(runs_kernel, out_shape=(vmem((rows, width), bf16), vmem((1...  158 us
    pallas_call x1, Pallas kernels, finish(): pl.pallas_call(finish_kernel, out_shape=shape((rows, width), bf16), in_sp...  3.39 us

profile of v6, /device:TPU:0, one launch (start us, length us, event | category | flops | bytes accessed | tf_op | source)
XLA Modules:
  0.0 161.8 jit_solution(11029587596841349040)
XLA Ops:
  0.0 0.0 copy-start.1
  0.0 157.5 %shard_map.39 = (bf16[2048,2048]{1,0:T(8,128)(2,1)S(1)}, f32[1,1]{1,0:T(1,128)}, f32[16,128]{1,0:T(8,128)S(1)}, f32[4,16,128]{2,1,0:T(8,128)S(1)}, f32[2048,256]...) custom-call(f32[16,128]{1,0:T(8,128)} %bitcast.3, ...), custom_call_target="tpu_custom_call" | custom-call | tf_op jit(solution)/shard_map/pallas_call | solution.py:743
  158.2 0.0 copy-done.1
  158.2 3.4 %conditional.1 = (bf16[2048,2048]{1,0:T(8,128)(2,1)}) conditional(s32[]{:T(128)} %bitcast.2, (bf16[2048,2048]{1,0:T(8,128)(2,1)S(1)}, f32[2048,256]{1,0:T(8,128)S(1)}, bf16[2048,256]{1,0:T(8,128)(2,1)S(1)}, bf16[768,256]{1,0:T(8,128)(2,1)S(1)}) %tuple.11, (f32[16,128]{1,0:T(8,128)S(1)}, bf16[2048,2048]{1,0:T(8,128)(2,1)}, f32[16,128]{1,0:T(8,128)S(1)}, ...), branch_computations={%region_0.0_spmd, %region_1.0_spmd} | conditional | bytes 33554468 | solution.py:773
  158.3 3.4 %branch_0_fun.1 = bf16[2048,2048]{1,0:T(8,128)(2,1)} custom-call(bf16[2048,2048]{1,0:T(8,128)(2,1)S(1)} %get-tuple-element.24.done_ref, f32[2048,256]{1,0:T(8,128)S(1)} %get-tuple-element.25.acc_ref, bf16[2048,256]{1,0:T(8,128)(2,1)S(1)} %get-tuple-element.26.end_mask, bf16[768,256]{1,0:T(8,128)(2,1)S(1)} %get-tuple-element.27.end_rows), custom_call_target="tpu_custom_call" | custom-call | tf_op jit(solution)/shard_map/cond/branch_0_fun/pallas_call | solution.py:725
Async XLA Ops:
  0.0 158.2 %copy-start.1 = (f32[2048]{0:T(1024)S(1)}, f32[2048]{0:T(1024)}, u32[]{:S(2)}) copy-start(f32[2048]{0:T(1024)} %param.5) | copy-start | bytes 24580

commit v7 on v5

--- a/solution.py
+++ b/solution.py
@@ -580,6 +580,7 @@
         @pl.when(i == 0)
         def _():
             receive(last, 4)
+            arrive(last, 3)
 
     tiles_loop(single_rows)
     take(last, 1)
@@ -587,7 +588,6 @@
     take(last, 2)
     receive(last, 3)
     loop(rows // tile, first_step)
-    arrive(last, 3)
     take(last, 3)
     arrive(last, 4)
     take(last, 4)
@@ -596,7 +596,7 @@
     for i, (buf, offset) in enumerate(((rows_buf, 0), (mid_buf, sums_at), (low_buf, sums_at))):
         end_rows[pl.ds(i * n, n), :] = buf[pl.ds(from_tile - offset, n), :]
     flag_all.wait()
-    flag_ref[...] = jnp.maximum(flags[2], flags[3])
+    flag_ref[...] = jnp.maximum(flags[2], flags[3])[0:1, 0:1]
     raw.wait_send()
     raw_fwd.wait_send()
     loop(chunks, lambda c: near(c).wait_send())
@@ -738,7 +738,7 @@
         small, kinds = 12, 5
         return pl.pallas_call(
             runs_kernel,
-            out_shape=(vmem((rows, width), bf16), vmem((8, LANES), f32), vmem(key_shape, f32),
+            out_shape=(vmem((rows, width), bf16), vmem((1, 1), f32), vmem(key_shape, f32),
                        vmem((4,) + key_shape, f32), vmem((rows, COL_W), f32),
                        vmem((rows, 4 * LANES), bf16), vmem((12 * LANES, COL_W), bf16),
                        shape((rows, width), bf16),

time: 162 us -> 161 us (level)
  no operation moved by 1% of the time
where the time goes in v7:
time: 161 us
  Pallas kernels  160 us (99%)
    pallas_call x1, Pallas kernels, run_exchange(): pl.pallas_call(runs_kernel, out_shape=(vmem((rows, width), bf16), vmem((1...  156 us
    pallas_call x1, Pallas kernels, finish(): pl.pallas_call(finish_kernel, out_shape=shape((rows, width), bf16), in_sp...  3.38 us

profile of v7, /device:TPU:0, one launch (start us, length us, event | category | flops | bytes accessed | tf_op | source)
XLA Modules:
  0.0 160.7 jit_solution(599899882797541427)
XLA Ops:
  0.0 0.0 copy-start.1
  0.0 156.4 %shard_map.39 = (bf16[2048,2048]{1,0:T(8,128)(2,1)S(1)}, f32[1,1]{1,0:T(1,128)}, f32[16,128]{1,0:T(8,128)S(1)}, f32[4,16,128]{2,1,0:T(8,128)S(1)}, f32[2048,256]...) custom-call(f32[16,128]{1,0:T(8,128)} %bitcast.3, ...), custom_call_target="tpu_custom_call" | custom-call | tf_op jit(solution)/shard_map/pallas_call | solution.py:739
  157.1 0.0 copy-done.1
  157.1 3.4 %conditional.1 = (bf16[2048,2048]{1,0:T(8,128)(2,1)}) conditional(s32[]{:T(128)} %bitcast.2, (bf16[2048,2048]{1,0:T(8,128)(2,1)S(1)}, f32[2048,256]{1,0:T(8,128)S(1)}, bf16[2048,512]{1,0:T(8,128)(2,1)S(1)}, bf16[1536,256]{1,0:T(8,128)(2,1)S(1)}) %tuple.11, (f32[16,128]{1,0:T(8,128)S(1)}, bf16[2048,2048]{1,0:T(8,128)(2,1)}, f32[16,128]{1,0:T(8,128)S(1)}, ...), branch_computations={%region_0.0_spmd, %region_1.0_spmd} | conditional | bytes 33554468 | solution.py:769
  157.1 3.4 %branch_0_fun.1 = bf16[2048,2048]{1,0:T(8,128)(2,1)} custom-call(bf16[2048,2048]{1,0:T(8,128)(2,1)S(1)} %get-tuple-element.24.done_ref, f32[2048,256]{1,0:T(8,128)S(1)} %get-tuple-element.25.acc_ref, bf16[2048,512]{1,0:T(8,128)(2,1)S(1)} %get-tuple-element.26.end_mask, bf16[1536,256]{1,0:T(8,128)(2,1)S(1)} %get-tuple-element.27.end_rows), custom_call_target="tpu_custom_call" | custom-call | tf_op jit(solution)/shard_map/cond/branch_0_fun/pallas_call | solution.py:721
Async XLA Ops:
  0.0 157.1 %copy-start.1 = (f32[2048]{0:T(1024)S(1)}, f32[2048]{0:T(1024)}, u32[]{:S(2)}) copy-start(f32[2048]{0:T(1024)} %param.5) | copy-start | bytes 24580

commit v8 on v7

--- a/solution.py
+++ b/solution.py
@@ -609,7 +609,7 @@
     rows, width = done_ref.shape
     n = end_mask.shape[1]
     done = pl.ds(0, width - COL_W)
-    pieces = 4
+    pieces = 16
     tile = rows // 2
 
     def store(i):
@@ -723,7 +723,7 @@
             out_shape=shape((rows, width), bf16),
             in_specs=[vmem_spec] * 4,
             out_specs=any_spec,
-            scratch_shapes=[vmem((rows, COL_W), bf16), dma((6,))],
+            scratch_shapes=[vmem((rows, COL_W), bf16), dma((18,))],
             compiler_params=pltpu.CompilerParams(vmem_limit_bytes=16000000),
         )(done, acc, end_mask, end_rows)
 

time: 161 us -> 162 us (level)
  no operation moved by 1% of the time
where the time goes in v8:
time: 162 us; the launch traced here: 161 us
  Pallas kernels  160 us (99%)
    pallas_call x1, Pallas kernels, run_exchange(): pl.pallas_call(runs_kernel, out_shape=(vmem((rows, width), bf16), vmem((1...  156 us
    pallas_call x1, Pallas kernels, finish(): pl.pallas_call(finish_kernel, out_shape=shape((rows, width), bf16), in_sp...  3.91 us

profile of v8, /device:TPU:0, one launch (start us, length us, event | category | flops | bytes accessed | tf_op | source)
XLA Modules:
  0.0 161.2 jit_solution(2429762442873761224)
XLA Ops:
  0.0 0.0 copy-start.1
  0.0 156.4 %shard_map.39 = (bf16[2048,2048]{1,0:T(8,128)(2,1)S(1)}, f32[1,1]{1,0:T(1,128)}, f32[16,128]{1,0:T(8,128)S(1)}, f32[4,16,128]{2,1,0:T(8,128)S(1)}, f32[2048,256]...) custom-call(f32[16,128]{1,0:T(8,128)} %bitcast.3, ...), custom_call_target="tpu_custom_call" | custom-call | tf_op jit(solution)/shard_map/pallas_call | solution.py:739
  157.1 0.0 copy-done.1
  157.1 3.9 %conditional.1 = (bf16[2048,2048]{1,0:T(8,128)(2,1)}) conditional(s32[]{:T(128)} %bitcast.2, (bf16[2048,2048]{1,0:T(8,128)(2,1)S(1)}, f32[2048,256]{1,0:T(8,128)S(1)}, bf16[2048,512]{1,0:T(8,128)(2,1)S(1)}, bf16[1536,256]{1,0:T(8,128)(2,1)S(1)}) %tuple.11, (f32[16,128]{1,0:T(8,128)S(1)}, bf16[2048,2048]{1,0:T(8,128)(2,1)}, f32[16,128]{1,0:T(8,128)S(1)}, ...), branch_computations={%region_0.0_spmd, %region_1.0_spmd} | conditional | bytes 33554468 | solution.py:769
  157.1 3.9 %branch_0_fun.1 = bf16[2048,2048]{1,0:T(8,128)(2,1)} custom-call(bf16[2048,2048]{1,0:T(8,128)(2,1)S(1)} %get-tuple-element.24.done_ref, f32[2048,256]{1,0:T(8,128)S(1)} %get-tuple-element.25.acc_ref, bf16[2048,512]{1,0:T(8,128)(2,1)S(1)} %get-tuple-element.26.end_mask, bf16[1536,256]{1,0:T(8,128)(2,1)S(1)} %get-tuple-element.27.end_rows), custom_call_target="tpu_custom_call" | custom-call | tf_op jit(solution)/shard_map/cond/branch_0_fun/pallas_call | solution.py:721
Async XLA Ops:
  0.0 157.1 %copy-start.1 = (f32[2048]{0:T(1024)S(1)}, f32[2048]{0:T(1024)}, u32[]{:S(2)}) copy-start(f32[2048]{0:T(1024)} %param.5) | copy-start | bytes 24580
